TPU v7x, 32 devices: a whole 2x2x4 slice. The times are simulated.
32 devices in a mesh: dp: 8 (over y, x, core), tensor: 4 (over z).
Axes of the slice: x: 2, y: 2, z: 4, core: 2. Of those that a mesh axis runs over, the one named last changes fastest.
Arguments:
- tokens: bfloat16 [4096, 1536], P('dp', 'tensor'), may hold values from -6 to 6
- cotangent: bfloat16 [4096, 1536], P('dp', 'tensor'), may hold values from -6 to 6
- seq_lens: int32 [8, 3], P('dp'), may hold values from 0 to 384, as said below
- input_norm_gain: float32 [1536], replicated, may hold values from 0.5 to 1.5
- w_zx: bfloat16 [1536, 2, 3072], P(None, None, 'tensor'), may hold values from -0.15625 to 0.15625
- w_bc: bfloat16 [1536, 256], replicated, may hold values from -0.15625 to 0.15625
- w_dt: bfloat16 [1536, 48], P(None, 'tensor'), may hold values from -0.078125 to 0.078125
- conv_wx: float32 [4, 3072], P(None, 'tensor'), may hold values from -3 to 3
- conv_bx: float32 [3072], P('tensor'), may hold values from -3 to 3
- conv_wbc: float32 [4, 256], replicated, may hold values from -3 to 3
- conv_bbc: float32 [256], replicated, may hold values from -3 to 3
- a_log: float32 [48], P('tensor'), may hold values from 0 to 2.7
- dt_bias: float32 [48], P('tensor'), may hold values from -6 to -2
- d_skip: float32 [48], P('tensor'), may hold values from 0.5 to 1.5
- norm_gate: float32 [3072], P('tensor'), may hold values from 0.5 to 1.5
- w_out: bfloat16 [3072, 1536], P('tensor'), may hold values from -0.109375 to 0.109375
Outputs:
- block_out: bfloat16 [4096, 1536], P('dp', 'tensor')
- d_tokens: float32 [4096, 1536], P('dp', 'tensor')
- grad_zx: float32 [1536, 2, 3072], P('dp', None, 'tensor')
- grad_bc: float32 [1536, 256], P('dp')
- grad_dt: float32 [1536, 48], P('dp', 'tensor')
- grad_out: float32 [3072, 1536], P('tensor', 'dp')
- grad_conv_wx: float32 [4, 3072], P(None, 'tensor')
- grad_conv_bx: float32 [3072], P('tensor')
- grad_conv_wbc: float32 [4, 256], replicated
- grad_conv_bbc: float32 [256], replicated
- grad_a_log: float32 [48], P('tensor')
- grad_dt_bias: float32 [48], P('tensor')
- grad_d_skip: float32 [48], P('tensor')
- grad_gate: float32 [3072], P('tensor')
- grad_in: float32 [1536], P('tensor')
Inputs may be any that keep to these rules, and one draw needn't show every extreme that they name: `seq_lens`: row d holds the lengths of the sequences packed in order from the first row of index d of dp; the rows after them are padding. Every row has exactly one length 384, its other lengths are at most 64, it sums to at most 512, and some row sums to exactly 512.
All inputs are finite; a program needn't handle non-finite values.
Results may differ from a plain program's by a relative error of at most 0.0076.
Values may be sent and summed in bfloat16 or wider, within the bound.
A program may use at most 192 MiB of HBM per device.

v0:
```python
from functools import partial

import jax
import jax.numpy as jnp
from jax import lax
from jax.sharding import PartitionSpec as P

D = 1536
SCAN_BLOCK = 256
INNER = 3072


NORM_EPS = 1e-05
PRECISE = lax.Precision.HIGHEST


def contract_rows(first_op, second_op):
    return lax.dot_general(
        first_op, second_op, (((0,), (0,)), ((), ())), preferred_element_type=jnp.float32
    )


def contract_cols(first_op, second_op):
    return lax.dot_general(
        first_op, second_op, (((1,), (1,)), ((), ())), preferred_element_type=jnp.float32
    )


def segment_ids(lengths, row_count):
    seq_ends = jnp.cumsum(lengths)
    positions = jnp.arange(row_count, dtype=jnp.int32)
    return jnp.sum((positions[:, None] >= seq_ends[None, :]).astype(jnp.int32), axis=1)


def causal_conv(signal, kernel_w, kernel_b, segment):
    kernel_len = kernel_w.shape[0]
    row_count = signal.shape[0]
    summed = kernel_b[None, :] + kernel_w[kernel_len - 1][None, :] * signal
    for lag_steps in range(1, kernel_len):
        shifted = jnp.concatenate(
            [jnp.zeros((lag_steps, signal.shape[1]), jnp.float32), signal[: row_count - lag_steps]],
            axis=0,
        )
        earlier = jnp.concatenate(
            [jnp.full((lag_steps,), -1, jnp.int32), segment[: row_count - lag_steps]]
        )
        same_seq = (earlier == segment).astype(signal.dtype)
        summed = (
            summed + kernel_w[kernel_len - 1 - lag_steps][None, :] * shifted * same_seq[:, None]
        )
    return summed


def ssd_scan(values, steps_dt, decay_rate, b_mat, c_mat, segment, block_len):
    row_count, heads_n, head_size = values.shape
    state_n = b_mat.shape[1]
    blocks_n = row_count // block_len
    log_decay = steps_dt * decay_rate[None, :]
    seg_lasts = segment[block_len - 1 :: block_len]
    prev_lasts = jnp.concatenate([jnp.full((1,), -1, jnp.int32), seg_lasts[:-1]])
    lower_tri = jnp.arange(block_len)[:, None] >= jnp.arange(block_len)[None, :]

    def blocked(source_arr):
        return source_arr.reshape((blocks_n, block_len) + source_arr.shape[1:])

    def one_block(carry_state, block_in):
        block_vals, block_decay, block_dt, block_b, block_c, block_seg, before_seg = block_in
        cumulated = jnp.cumsum(block_decay, axis=0)
        same_seq = ((block_seg[:, None] == block_seg[None, :]) & lower_tri)[:, :, None]
        log_gaps = cumulated[:, None, :] - cumulated[None, :, :]
        decays = jnp.where(same_seq, jnp.exp(jnp.where(same_seq, log_gaps, 0.0)), 0.0)
        scores = jnp.einsum("in,jn->ij", block_c, block_b, precision=PRECISE)
        mixing = decays * scores[:, :, None] * block_dt[None, :, :]
        intra_out = jnp.einsum("ijh,jhp->ihp", mixing, block_vals, precision=PRECISE)
        keep_in = (block_seg == before_seg).astype(block_vals.dtype)
        entering = jnp.exp(cumulated) * keep_in[:, None]
        inter_out = (
            jnp.einsum("in,hnp->ihp", block_c, carry_state, precision=PRECISE)
            * entering[:, :, None]
        )
        tail_in = (block_seg == block_seg[-1]).astype(block_vals.dtype)
        to_end = jnp.exp(cumulated[-1][None, :] - cumulated) * tail_in[:, None] * block_dt
        carried = carry_state * (jnp.exp(cumulated[-1]) * keep_in[-1])[:, None, None]
        new_state = carried + jnp.einsum(
            "jh,jn,jhp->hnp", to_end, block_b, block_vals, precision=PRECISE
        )
        return (new_state, intra_out + inter_out)

    init_state = jnp.zeros((heads_n, state_n, head_size), values.dtype)
    inputs = (
        blocked(values),
        blocked(log_decay),
        blocked(steps_dt),
        blocked(b_mat),
        blocked(c_mat),
        blocked(segment),
        prev_lasts,
    )
    scan_out = lax.scan(one_block, init_state, inputs)[1]
    return scan_out.reshape(row_count, heads_n, head_size)


def mixer_core(
    zx_rows,
    dt_raw,
    b_conv,
    c_conv,
    conv_wx,
    conv_bx,
    a_log,
    dt_bias,
    d_skip,
    segment=None,
    heads_n=1,
):
    inner_n = zx_rows.shape[1] // 2
    row_count = zx_rows.shape[0]
    x_conv = jax.nn.silu(causal_conv(zx_rows[:, inner_n:], conv_wx, conv_bx, segment))
    steps_dt = jax.nn.softplus(dt_raw + dt_bias[None, :])
    decay_rate = -jnp.exp(a_log)
    values = x_conv.reshape(row_count, heads_n, inner_n // heads_n)
    mixed_out = (
        ssd_scan(values, steps_dt, decay_rate, b_conv, c_conv, segment, SCAN_BLOCK)
        + d_skip[None, :, None] * values
    )
    return mixed_out.reshape(row_count, inner_n) * jax.nn.silu(zx_rows[:, :inner_n])


def bc_core(bc_pre, conv_wbc, conv_bbc, segment=None):
    return jax.nn.silu(causal_conv(bc_pre, conv_wbc, conv_bbc, segment))


def per_device(
    tokens,
    cotangent,
    seq_lens,
    input_norm_gain,
    w_zx,
    w_bc,
    w_dt,
    conv_wx,
    conv_bx,
    conv_wbc,
    conv_bbc,
    a_log,
    dt_bias,
    d_skip,
    norm_gate,
    w_out,
):
    x_full, cot_full = (
        lax.all_gather(tokens, "tensor", axis=1, tiled=True),
        lax.all_gather(cotangent, "tensor", axis=1, tiled=True),
    )
    row_count = tokens.shape[0]
    feat_n = tokens.shape[1]
    feat_start = lax.axis_index("tensor") * feat_n
    state_n = w_bc.shape[1] // 2
    inner_loc = norm_gate.shape[0]
    segment = segment_ids(seq_lens[0], row_count)
    is_live = (segment < seq_lens.shape[1])[:, None]
    w_zx_flat = w_zx.reshape(D, 2 * inner_loc)
    tok_float = x_full.astype(jnp.float32)
    inverse_root_mean = lax.rsqrt(jnp.mean(tok_float * tok_float, axis=1, keepdims=True) + NORM_EPS)
    unit_scaled_input = tok_float * inverse_root_mean
    normed = (unit_scaled_input * input_norm_gain[None, :]).astype(jnp.bfloat16)
    zx_rows = jnp.dot(normed, w_zx_flat, preferred_element_type=jnp.float32)
    bc_pre = jnp.dot(normed, w_bc, preferred_element_type=jnp.float32)
    dt_raw = jnp.dot(normed, w_dt, preferred_element_type=jnp.float32)
    bc_post, bc_back = jax.vjp(partial(bc_core, segment=segment), bc_pre, conv_wbc, conv_bbc)
    gated_rows, core_back = jax.vjp(
        partial(mixer_core, segment=segment, heads_n=a_log.shape[0]),
        zx_rows,
        dt_raw,
        bc_post[:, :state_n],
        bc_post[:, state_n:],
        conv_wx,
        conv_bx,
        a_log,
        dt_bias,
        d_skip,
    )
    cot_live = jnp.where(is_live, cot_full, jnp.zeros_like(cot_full))
    d_gate = contract_cols(cot_live, w_out)
    d_hat = d_gate * norm_gate[None, :]
    squares, cross_sum = lax.psum(
        (
            jnp.sum(gated_rows * gated_rows, axis=1, keepdims=True),
            jnp.sum(d_hat * gated_rows, axis=1, keepdims=True),
        ),
        "tensor",
    )
    r_gate = lax.rsqrt(squares / INNER + NORM_EPS)
    gate_hat = gated_rows * r_gate
    gate_out = (gate_hat * norm_gate[None, :]).astype(jnp.bfloat16)
    branch_part = jnp.dot(gate_out, w_out, preferred_element_type=jnp.float32)
    branch = lax.psum_scatter(branch_part, "tensor", scatter_dimension=1, tiled=True)
    own_float = tokens.astype(jnp.float32)
    block_out = (own_float + jnp.where(is_live, branch, 0.0)).astype(jnp.bfloat16)
    grad_out = contract_rows(gate_out, cot_live)
    grad_gate = jnp.sum(d_gate * gate_hat, axis=0)
    d_gated = r_gate * d_hat - gated_rows * (r_gate * r_gate * r_gate * cross_sum / INNER)
    d_zx, d_dt, d_b, d_c, grad_conv_wx, grad_conv_bx, grad_a_log, grad_dt_bias, grad_d_skip = (
        core_back(d_gated)
    )
    d_bc_post = lax.psum(jnp.concatenate([d_b, d_c], axis=1), "tensor")
    d_bc, grad_conv_wbc, grad_conv_bbc = bc_back(d_bc_post)
    d_zx_half = d_zx.astype(jnp.bfloat16)
    d_bc_half = d_bc.astype(jnp.bfloat16)
    d_dt_half = d_dt.astype(jnp.bfloat16)
    grad_zx = contract_rows(normed, d_zx_half)
    grad_bc = contract_rows(normed, d_bc_half)
    grad_dt = contract_rows(normed, d_dt_half)
    partial_in = contract_cols(d_zx_half, w_zx_flat) + contract_cols(d_dt_half, w_dt)
    own_hat = lax.dynamic_slice_in_dim(unit_scaled_input, feat_start, feat_n, 1)
    own_gain = lax.dynamic_slice_in_dim(input_norm_gain, feat_start, feat_n, 0)
    normed_input_gradient = lax.psum(partial_in, "tensor") + contract_cols(d_bc_half, w_bc)
    unit_input_gradient = normed_input_gradient * input_norm_gain[None, :]
    row_inner_product = jnp.mean(unit_input_gradient * unit_scaled_input, axis=1, keepdims=True)
    own_dn = lax.dynamic_slice_in_dim(normed_input_gradient, feat_start, feat_n, 1)
    own_dxhat = own_dn * own_gain[None, :]
    grad_in = jnp.sum(own_dn * own_hat, axis=0)
    d_tokens = cotangent.astype(jnp.float32) + inverse_root_mean * (
        own_dxhat - own_hat * row_inner_product
    )
    grad_zx_sum, grad_bc_sum, grad_dt_sum, grad_out_sum = (
        lax.psum_scatter(grad_zx, "dp", scatter_dimension=0, tiled=True),
        lax.psum_scatter(grad_bc, "dp", scatter_dimension=0, tiled=True),
        lax.psum_scatter(grad_dt, "dp", scatter_dimension=0, tiled=True),
        lax.psum_scatter(grad_out, "dp", scatter_dimension=1, tiled=True),
    )
    smalls = lax.psum(
        (
            grad_conv_wx,
            grad_conv_bx,
            grad_conv_wbc,
            grad_conv_bbc,
            grad_a_log,
            grad_dt_bias,
            grad_d_skip,
            grad_gate,
            grad_in,
        ),
        "dp",
    )
    grad_zx_out = grad_zx_sum.reshape(grad_zx_sum.shape[0], 2, inner_loc)
    return (
        block_out,
        d_tokens,
        grad_zx_out,
        grad_bc_sum,
        grad_dt_sum,
        grad_out_sum,
        smalls[0],
        smalls[1],
        smalls[2],
        smalls[3],
        smalls[4],
        smalls[5],
        smalls[6],
        smalls[7],
        smalls[8],
    )


def solution(mesh):
    in_specs = (
        P("dp", "tensor"),
        P("dp", "tensor"),
        P("dp", None),
        P(),
        P(None, None, "tensor"),
        P(),
        P(None, "tensor"),
        P(None, "tensor"),
        P("tensor"),
        P(),
        P(),
        P("tensor"),
        P("tensor"),
        P("tensor"),
        P("tensor"),
        P("tensor", None),
    )
    out_specs = (
        P("dp", "tensor"),
        P("dp", "tensor"),
        P("dp", None, "tensor"),
        P("dp", None),
        P("dp", "tensor"),
        P("tensor", "dp"),
        P(None, "tensor"),
        P("tensor"),
        P(),
        P(),
        P("tensor"),
        P("tensor"),
        P("tensor"),
        P("tensor"),
        P("tensor"),
    )
    return jax.shard_map(
        per_device, mesh=mesh, in_specs=in_specs, out_specs=out_specs, check_vma=False
    )
```

profile of v0, /device:TPU:0, one launch (start us, length us, event | category | flops | bytes accessed | tf_op | source)
XLA Modules:
  0.0 829.0 jit_solution(16119154186207128450)
XLA Ops:
  10.0 5.4 copy.202
  16.9 32.0 %all-gather.3.cloned.1.call-done = bf16[512,1536]{1,0:T(8,128)(2,1)} async-done(((bf16[512,384]{1,0:T(8,128)(2,1)}), bf16[512,1536]{1,0:T(8,128)(2,1)}) %all-gather.3.cloned.1.call-update) | async-done | bytes 1572880 | tf_op jit(solution)/shard_map/all_gather | solution.py:152
  50.9 4.6 fusion.165
  58.2 2.9 fusion.137
  61.1 3.0 copy.128
  64.1 3.1 reshape.497
  67.2 3.0 copy.131
  77.3 106.6 %while.83 = (s32[]{:T(128)}, f32[12,128,64]{1,2,0:T(8,128)}, f32[2,256,12,64]{1,0,3,2:T(2,128)}, pred[2,256,256,12]{2,1,3,0:T(32,128)(4,1)}, f32[2,256,256,12]{2...) while((s32[]{:T(128)}, f32[12,128,64]{1,2,0:T(8,128)}, ...), condition=%wide.region_6.7_spmd.clone, body=%wide.region_3.6_spmd.clone.sunk | while | flops 1318172672 | bytes 44319708 | solution.py:99
  89.8 5.1 multiply_dynamic-update-slice_fusion.2
  98.1 3.7 fusion.232
  103.5 16.8 %dynamic_update_slice.292 = f32[2,256,12,64]{1,0,3,2:T(2,128)} dynamic-update-slice(f32[2,256,12,64]{1,0,3,2:T(2,128)} %get-tuple-element.2383, f32[1,256,12,64]{1,0,3,2:T(1,128)} %copy.250, s32[]{:T(128)} %get-tuple-element.2381, s32[]{:T(128)} %constant.210.clone.1..sunk, s32[]{:T(128)} %constant.210.clone.1..sunk, s32[]{:T(128)} %constant.210.clone.1..sunk) | dynamic-update-slice | bytes 1572868 | tf_op jit(solution)/shard_map/jvp()/while/body/jit(dynamic_update_index_in_dim)/dynamic_update_slice | solution.py:99
  120.3 2.8 bitcast_dynamic-update-slice_fusion.20
  123.8 2.4 fusion.229
  142.3 5.1 multiply_dynamic-update-slice_fusion.2
  151.7 3.7 fusion.232
  157.2 16.8 %dynamic_update_slice.292 = f32[2,256,12,64]{1,0,3,2:T(2,128)} dynamic-update-slice(f32[2,256,12,64]{1,0,3,2:T(2,128)} %get-tuple-element.2383, f32[1,256,12,64]{1,0,3,2:T(1,128)} %copy.250, s32[]{:T(128)} %get-tuple-element.2381, s32[]{:T(128)} %constant.210.clone.1..sunk, s32[]{:T(128)} %constant.210.clone.1..sunk, s32[]{:T(128)} %constant.210.clone.1..sunk) | dynamic-update-slice | bytes 1572868 | tf_op jit(solution)/shard_map/jvp()/while/body/jit(dynamic_update_index_in_dim)/dynamic_update_slice | solution.py:99
  174.0 2.8 bitcast_dynamic-update-slice_fusion.20
  177.5 2.5 fusion.229
  183.8 2.7 copy.203
  186.6 3.0 copy.133
  189.6 4.3 multiply_reduce_fusion.9
  193.9 10.0 %psum.91 = f32[512,1]{0,1:T(1,128)S(1)} all-reduce(f32[512,1]{0,1:T(1,128)S(1)} %bitcast.544), channel_id=1, replica_groups=mesh['dp'=8,'tensor'=4] {'tensor'}, use_global_device_ids=true, to_apply=%region_8.9 | all-reduce | flops 512 | bytes 4096 | tf_op jit(solution)/shard_map/psum | solution.py:186
  204.0 5.1 multiply_reduce_fusion.2
  209.1 8.7 %psum.92 = f32[512,1]{0,1:T(1,128)S(1)} all-reduce(f32[512,1]{0,1:T(1,128)S(1)} %bitcast.550), channel_id=1, replica_groups=mesh['dp'=8,'tensor'=4] {'tensor'}, use_global_device_ids=true, to_apply=%region_11.12 | all-reduce | flops 512 | bytes 4096 | tf_op jit(solution)/shard_map/psum | solution.py:186
  217.8 5.8 multiply_reduce_fusion.3
  223.6 3.1 copy.134
  226.7 3.1 reshape.501
  234.2 146.2 %while.84 = (s32[]{:T(128)}, f32[12,128,64]{1,2,0:T(8,128)S(1)}, f32[2,256,12,64]{1,0,3,2:T(2,128)}, f32[2,256,12]{1,0,2:T(2,128)}, f32[2,256,12]{1,0,2:T(2,128)...) while((s32[]{:T(128)}, f32[12,128,64]{1,2,0:T(8,128)S(1)}, ...), condition=%wide.region_22.23_spmd.clone, body=%wide.region_12.22_spmd.clone.sunk | while | flops 2628679680 | bytes 40395960 | solution.py:99
  234.6 2.3 constant_dynamic-slice_fusion.11
  238.0 7.7 fusion.249
  245.7 2.9 fusion.247
  262.9 3.2 reduce-window.59
  271.0 4.1 fusion.248
  276.8 16.8 %dynamic_update_slice.296 = f32[2,256,12,64]{1,0,3,2:T(2,128)} dynamic-update-slice(f32[2,256,12,64]{1,0,3,2:T(2,128)} %get-tuple-element.2486, f32[1,256,12,64]{1,0,3,2:T(1,128)} %copy.256, s32[]{:T(128)S(6)} %sub.239, s32[]{:T(128)} %constant.210.clone.1..sunk.1, s32[]{:T(128)} %constant.210.clone.1..sunk.1, s32[]{:T(128)} %constant.210.clone.1..sunk.1) | dynamic-update-slice | bytes 1572868 | tf_op jit(solution)/shard_map/transpose(jvp())/while/body/jit(dynamic_update_index_in_dim)/dynamic_update_slice | solution.py:99
  294.3 2.4 convolution_bitcast_fusion.7
  300.8 2.5 convolution_bitcast_fusion.6
  303.3 2.2 fusion.254
  307.4 2.3 constant_dynamic-slice_fusion.11
  310.8 7.7 fusion.249
  318.5 2.9 fusion.247
  335.8 3.2 reduce-window.59
  343.8 4.1 fusion.248
  349.7 16.8 %dynamic_update_slice.296 = f32[2,256,12,64]{1,0,3,2:T(2,128)} dynamic-update-slice(f32[2,256,12,64]{1,0,3,2:T(2,128)} %get-tuple-element.2486, f32[1,256,12,64]{1,0,3,2:T(1,128)} %copy.256, s32[]{:T(128)S(6)} %sub.239, s32[]{:T(128)} %constant.210.clone.1..sunk.1, s32[]{:T(128)} %constant.210.clone.1..sunk.1, s32[]{:T(128)} %constant.210.clone.1..sunk.1) | dynamic-update-slice | bytes 1572868 | tf_op jit(solution)/shard_map/transpose(jvp())/while/body/jit(dynamic_update_index_in_dim)/dynamic_update_slice | solution.py:99
  367.2 2.4 convolution_bitcast_fusion.7
  373.6 2.5 convolution_bitcast_fusion.6
  376.2 2.2 fusion.254
  381.9 2.7 copy.204
  384.6 3.1 copy.139
  387.8 3.9 multiply_reduce_fusion.7
  399.0 2.6 fusion.146
  401.9 2.3 convolution_add_fusion.2
  404.8 3.0 fusion.150
  408.0 4.9 fusion.162
  412.9 8.7 %fusion.145 = f32[1536,1536]{1,0:T(8,128)} fusion(f32[512,768]{1,0:T(8,128)} %copy-done.19, f32[512,768]{1,0:T(8,128)} %get-tuple-element.1867, f32[1536]{0:T(1024)S(1)} %copy-done.67, f32[512]{0:T(512)S(1)} %copy-done.64, bf16[512,1536]{1,0:T(8,128)(2,1)} %all-gather.3.cloned.1.call-done), kind=kOutput, calls=%fused_computation.248 | convolution fusion | flops 2420637696 | bytes 14163968 | tf_op jit(solution)/shard_map/dot_general | solution.py:18
  421.9 119.7 %all-reduce.30.cloned.1.call-done = (f32[512,1536]{1,0:T(8,128)}, f32[512,256]{1,0:T(8,128)}) async-done(((f32[512,1536]{1,0:T(8,128)}, f32[512,256]{1,0:T(8,128)}), (f32[512,1536]{1,0:T(8,128)}, f32[512,256]{1,0:T(8,128)})) %all-reduce.30.cloned.1.call-update) | async-done | bytes 3670032 | tf_op jit(solution)/shard_map/psum | solution.py:217
  548.3 5.7 fusion.139
  554.9 24.2 %reduce-scatter.16.cloned.1.call-done = f32[192,12]{1,0:T(8,128)} async-done(((f32[1536,12]{1,0:T(8,128)}), f32[192,12]{1,0:T(8,128)}) %reduce-scatter.16.cloned.1.call-update) | async-done | bytes 9232
  580.8 3.6 multiply_reduce_fusion.1
  585.6 23.7 %all-reduce.26 = (f32[4,768]{1,0:T(4,128)}, f32[768]{0:T(1024)}, f32[4,256]{1,0:T(4,128)}, f32[256]{0:T(256)}, f32[12]{0:T(128)}, /*index=5*/f32[12]{0:T(128)}, f32[12]{0:T(128)}, f32[768]{0:T(1024)}, f32[384]{0:T(512)}) all-reduce(f32[4,768]{1,0:T(4,128)S(1)} %pad_add_fusion, ...), channel_id=1, replica_groups=mesh['dp'=8,'tensor'=4] {'dp'}, use_global_device_ids=true, to_apply=%region_34.35 | all-reduce | flops 6308 | bytes 50464 | tf_op jit(solution)/shard_map/psum | solution.py:232
  609.3 32.4 %reduce-scatter.8.cloned.1.call-done = f32[512,384]{1,0:T(8,128)} async-done(((f32[512,1536]{1,0:T(8,128)}), f32[512,384]{1,0:T(8,128)}) %reduce-scatter.8.cloned.1.call-update) | async-done | bytes 786448 | tf_op jit(solution)/shard_map/reduce_scatter | solution.py:197
  643.8 78.0 %reduce-scatter.10.cloned.1.call-done = f32[192,1536]{1,0:T(8,128)} async-done(((f32[1536,1536]{1,0:T(8,128)}), f32[192,1536]{1,0:T(8,128)}) %reduce-scatter.10.cloned.1.call-update) | async-done | bytes 1179664 | tf_op jit(solution)/shard_map/reduce_scatter | solution.py:227
  721.9 3.0 reshape.507
  724.8 39.3 %reduce-scatter.12.cloned.1.call-done = f32[192,256]{1,0:T(8,128)} async-done(((f32[1536,256]{1,0:T(8,128)}), f32[192,256]{1,0:T(8,128)}) %reduce-scatter.12.cloned.1.call-update) | async-done | bytes 196624 | tf_op jit(solution)/shard_map/reduce_scatter | solution.py:228
  764.1 57.9 %reduce-scatter.14.cloned.1.call-done = f32[768,192]{0,1:T(8,128)} async-done(((f32[768,1536]{0,1:T(8,128)}), f32[768,192]{0,1:T(8,128)}) %reduce-scatter.14.cloned.1.call-update) | async-done | bytes 589840 | tf_op jit(solution)/shard_map/reduce_scatter | solution.py:230
  (463 shorter events, 143.6 us)
Async XLA Ops:
  7.2 196.8 %copy-start = (bf16[768,1536]{1,0:T(8,128)(2,1)S(1)}, bf16[768,1536]{1,0:T(8,128)(2,1)}, u32[]{:S(2)}) copy-start(bf16[768,1536]{1,0:T(8,128)(2,1)} %param.35) | copy-start | bytes 7077892
  7.2 41.7 %all-gather.3.cloned.1.call-start = ((), (), s32[]{:S(2)}) async-start(), calls=%async_computation.5 | async-start | bytes 1966080 | tf_op jit(solution)/shard_map/all_gather | solution.py:152
  7.9 196.0 %all-gather.5.cloned.1.call-start = ((), (), s32[]{:S(2)}) async-start(), calls=%async_computation.7 | async-start | bytes 1966080 | tf_op jit(solution)/shard_map/all_gather | solution.py:153
  8.7 533.0 %all-reduce.30.cloned.1.call-start = ((), (), s32[]{:S(2)}) async-start(), calls=%async_computation.12 | async-start | bytes 7340032 | tf_op jit(solution)/shard_map/psum | solution.py:217
  9.9 5.5 copy-start.69
  9.9 5.5 copy-start.82
  9.9 5.6 copy-start.88
  9.9 5.6 copy-start.86
  15.4 35.5 %copy-start.66 = (f32[1536]{0:T(1024)S(1)}, f32[1536]{0:T(1024)}, u32[]{:S(2)}) copy-start(f32[1536]{0:T(1024)} %param.23) | copy-start | bytes 18436
  15.4 40.4 %copy-start.52 = (f32[768]{0:T(1024)}, f32[768]{0:T(1024)S(1)}, u32[]{:S(2)}) copy-start(f32[768]{0:T(1024)S(1)} %get-tuple-element.1672) | copy-start | bytes 9220
  15.5 40.4 %copy-start.54 = (f32[768]{0:T(1024)}, f32[768]{0:T(1024)S(1)}, u32[]{:S(2)}) copy-start(f32[768]{0:T(1024)S(1)} %get-tuple-element.1674) | copy-start | bytes 9220
  15.5 40.4 %copy-start.56 = (f32[768]{0:T(1024)}, f32[768]{0:T(1024)S(1)}, u32[]{:S(2)}) copy-start(f32[768]{0:T(1024)S(1)} %get-tuple-element.1673) | copy-start | bytes 9220
  15.5 40.4 %copy-start.58 = (f32[768]{0:T(1024)}, f32[768]{0:T(1024)S(1)}, u32[]{:S(2)}) copy-start(f32[768]{0:T(1024)S(1)} %get-tuple-element.1675) | copy-start | bytes 9220
  15.5 55.3 %copy-start.70 = (f32[1,256]{1,0:T(1,128)}, f32[1,256]{1,0:T(1,128)S(1)}, u32[]{:S(2)}) copy-start(f32[1,256]{1,0:T(1,128)S(1)} %get-tuple-element.1883) | copy-start | bytes 3076
  15.5 55.3 %copy-start.72 = (f32[1,256]{1,0:T(1,128)}, f32[1,256]{1,0:T(1,128)S(1)}, u32[]{:S(2)}) copy-start(f32[1,256]{1,0:T(1,128)S(1)} %get-tuple-element.1885) | copy-start | bytes 3076
  15.5 55.3 %copy-start.74 = (f32[1,256]{1,0:T(1,128)}, f32[1,256]{1,0:T(1,128)S(1)}, u32[]{:S(2)}) copy-start(f32[1,256]{1,0:T(1,128)S(1)} %get-tuple-element.1884) | copy-start | bytes 3076
  15.5 55.3 %copy-start.76 = (f32[1,256]{1,0:T(1,128)}, f32[1,256]{1,0:T(1,128)S(1)}, u32[]{:S(2)}) copy-start(f32[1,256]{1,0:T(1,128)S(1)} %get-tuple-element.1886) | copy-start | bytes 3076
  15.6 57.4 %copy-start.84 = (f32[12]{0:T(128)}, f32[12]{0:T(128)S(1)}, u32[]{:S(2)}) copy-start(f32[12]{0:T(128)S(1)} %exponential_negate_fusion) | copy-start | bytes 148
  15.7 202.1 %copy-start.38 = (f32[768]{0:T(1024)}, f32[768]{0:T(1024)S(1)}, u32[]{:S(2)}) copy-start(f32[768]{0:T(1024)S(1)} %mul.1008) | copy-start | bytes 9220
  16.9 54.0 %copy-start.42 = (f32[512]{0:T(512)}, f32[512]{0:T(512)S(1)}, u32[]{:S(2)}) copy-start(f32[512]{0:T(512)S(1)} %get-tuple-element.1888) | copy-start | bytes 6148
  16.9 54.0 %copy-start.44 = (f32[512]{0:T(512)}, f32[512]{0:T(512)S(1)}, u32[]{:S(2)}) copy-start(f32[512]{0:T(512)S(1)} %get-tuple-element.1889) | copy-start | bytes 6148
  16.9 54.0 %copy-start.46 = (f32[512]{0:T(512)}, f32[512]{0:T(512)S(1)}, u32[]{:S(2)}) copy-start(f32[512]{0:T(512)S(1)} %get-tuple-element.1890) | copy-start | bytes 6148
  50.9 22.2 %copy-start.63 = (f32[512]{0:T(512)}, f32[512]{0:T(512)S(1)}, u32[]{:S(2)}) copy-start(f32[512]{0:T(512)S(1)} %add_rsqrt_fusion.1) | copy-start | bytes 6148
  55.9 5.3 copy-start.13
  77.4 7.4 copy-start.50
  86.2 8.7 %copy-start.40 = (f32[12]{0:T(128)}, f32[12]{0:T(128)S(1)}, u32[]{:S(2)}) copy-start(f32[12]{0:T(128)S(1)} %get-tuple-element.2281) | copy-start | bytes 148 | tf_op jit(solution)/shard_map/jvp()/while
  98.0 3.8 copy-start.4
  120.3 3.5 copy-start.2
  123.1 5.7 copy-start.32
  123.1 7.0 copy-start.51
  130.1 7.3 copy-start.50
  138.7 8.7 %copy-start.40 = (f32[12]{0:T(128)}, f32[12]{0:T(128)S(1)}, u32[]{:S(2)}) copy-start(f32[12]{0:T(128)S(1)} %get-tuple-element.2281) | copy-start | bytes 148 | tf_op jit(solution)/shard_map/jvp()/while
  148.1 3.7 copy-start.1
  151.7 3.8 copy-start.4
  173.9 3.6 copy-start.2
  176.8 5.7 copy-start.32
  176.8 7.0 copy-start.51
  189.6 14.4 %copy-start.35 = (f32[768]{0:T(1024)S(1)}, f32[768]{0:T(1024)}, u32[]{:S(2)}) copy-start(f32[768]{0:T(1024)} %param.34) | copy-start | bytes 9220
  189.6 14.4 %copy-start.78 = (pred[512]{0:T(512)(128)(4,1)S(1)}, pred[512]{0:T(512)(128)(4,1)}, u32[]{:S(2)}) copy-start(pred[512]{0:T(512)(128)(4,1)} %get-tuple-element.1887) | copy-start | bytes 1540
  204.0 13.9 %copy-start.60 = (f32[512,1]{0,1:T(1,128)}, f32[512,1]{0,1:T(1,128)S(1)}, u32[]{:S(2)}) copy-start(f32[512,1]{0,1:T(1,128)S(1)} %add_rsqrt_fusion) | copy-start | bytes 6148
  234.6 3.4 copy-start.3
  245.7 4.1 copy-start.29
  293.6 5.2 copy-start.18
  300.8 4.8 copy-start.92
  307.4 3.4 copy-start.3
  318.5 4.2 copy-start.29
  366.4 5.2 copy-start.18
  373.6 4.8 copy-start.92
  387.7 3.9 copy-start.10
  387.7 3.9 copy-start.12
  387.7 3.9 copy-start.45
  387.7 3.9 copy-start.47
  396.4 5.3 copy-start.19
  404.2 3.8 copy-start.36
  404.2 3.8 copy-start.61
  404.2 175.0 %reduce-scatter.16.cloned.1.call-start = ((), (), s32[]{:S(2)}) async-start(), calls=%async_computation.11 | async-start | bytes 884736
  407.9 233.9 %reduce-scatter.8.cloned.1.call-start = ((), (), s32[]{:S(2)}) async-start(), calls=%async_computation.6 | async-start | bytes 3932160 | tf_op jit(solution)/shard_map/reduce_scatter | solution.py:197
  412.9 309.0 %reduce-scatter.10.cloned.1.call-start = ((), (), s32[]{:S(2)}) async-start(), calls=%async_computation.8 | async-start | bytes 10616832 | tf_op jit(solution)/shard_map/reduce_scatter | solution.py:227
  421.7 120.0 %copy-start.8 = (f32[512,256]{1,0:T(8,128)S(1)}, f32[512,256]{1,0:T(8,128)}, u32[]{:S(2)}) copy-start(f32[512,256]{1,0:T(8,128)} %copy-done.7) | copy-start | bytes 1572868
  421.7 120.0 %copy-start.17 = (f32[512,256]{1,0:T(8,128)S(1)}, f32[512,256]{1,0:T(8,128)}, u32[]{:S(2)}) copy-start(f32[512,256]{1,0:T(8,128)} %get-tuple-element.1843) | copy-start | bytes 1572868
  421.7 342.4 %reduce-scatter.12.cloned.1.call-start = ((), (), s32[]{:S(2)}) async-start(), calls=%async_computation.9 | async-start | bytes 1769472 | tf_op jit(solution)/shard_map/reduce_scatter | solution.py:228
  547.7 274.3 %reduce-scatter.14.cloned.1.call-start = ((), (), s32[]{:S(2)}) async-start(), calls=%async_computation.10 | async-start | bytes 5308416 | tf_op jit(solution)/shard_map/reduce_scatter | solution.py:230
  580.8 3.7 copy-start.20
  584.4 57.4 %copy-start.21 = (bf16[512,384]{1,0:T(8,128)(2,1)S(1)}, bf16[512,384]{1,0:T(8,128)(2,1)}, u32[]{:S(2)}) copy-start(bf16[512,384]{1,0:T(8,128)(2,1)} %param.20) | copy-start | bytes 1179652
  (62 other events, 128.7 us)
Sparse Core Ops, SparseCore 0:
  9.6 39.3 all-gather.2
  50.5 35.9 all-gather.4
  404.3 137.2 all-reduce.29
  545.2 33.9 reduce-scatter.15
  581.3 60.4 reduce-scatter.7
  645.1 76.6 reduce-scatter.9
  725.7 38.3 reduce-scatter.11
  768.1 53.7 reduce-scatter.13
where the time goes:
time: 843 us; the launch traced here: 829 us
  waiting for transfers between devices  385 us (46%)
  local copies, waits for them, and re-layouts  178 us (21%)
  matrix products  116 us (14%)
  other arithmetic  90.7 us (11%)
  blocking collectives  42.4 us (5%)
  between operations  15.3 us (2%)
    psum x1, waiting for transfers between devices, per_device(): lax.psum(partial_in, 'tensor') + contract_cols(d_bc_half, w_bc)  120 us
    dynamic_update_slice x26, local copies, waits for them, and re-layouts, ssd_scan(): scan_out = lax.scan(one_block, init_state, inputs)[1]  87.3 us
    reduce_scatter x1, waiting for transfers between devices, per_device(): lax.psum_scatter(grad_zx, 'dp', scatter_dimension=0, tiled=True)  78 us
    reduce_scatter x1, waiting for transfers between devices, per_device(): lax.psum_scatter(grad_out, 'dp', scatter_dimension=1, tiled=True)  57.9 us
    reduce_scatter x1, waiting for transfers between devices, per_device(): lax.psum_scatter(grad_bc, 'dp', scatter_dimension=0, tiled=True)  39.3 us
    reduce_scatter x1, waiting for transfers between devices, per_device(): lax.psum_scatter(branch_part, 'tensor', scatter_dimension=1, tiled=True)  32.4 us
    all_gather x1, waiting for transfers between devices, per_device(): lax.all_gather(tokens, 'tensor', axis=1, tiled=True)  32 us
    dot_general x6, matrix products, one_block(): jnp.einsum('ijh,jhp->ihp', mixing, block_vals, precision=PRECISE)  31.2 us
  transfers between devices with their start and end apart: 8, of which 7 were waited for; matrix products, arithmetic and copies ran while one was open for 22% of the time, Pallas kernels for 0%

commit v1 on v0

v1 whole, which is shorter than its diff:
```python
from functools import partial


import jax
import jax.numpy as jnp
from jax import lax
from jax.experimental import pallas as pl
from jax.experimental.pallas import tpu as pltpu

PRECISE = lax.Precision.HIGHEST
HEAD_DIM = 64
PAIR = 2


def _dot(a, b):
    return jnp.dot(a, b, precision=PRECISE, preferred_element_type=jnp.float32)


def _dot_tn(a, b):
    return lax.dot_general(a, b, (((0,), (0,)), ((), ())), precision=PRECISE,
                           preferred_element_type=jnp.float32)


def _dot_nt(a, b):
    return lax.dot_general(a, b, (((1,), (1,)), ((), ())), precision=PRECISE,
                           preferred_element_type=jnp.float32)


def _prologue(c_ref, b_ref, segc_ref, segr_ref, s_scr, neg_scr):
    s_scr[...] = _dot_nt(c_ref[...], b_ref[...])
    rows = s_scr.shape[0]
    row_i = lax.broadcasted_iota(jnp.int32, (rows, rows), 0)
    col_j = lax.broadcasted_iota(jnp.int32, (rows, rows), 1)
    keep = (col_j <= row_i) & (segc_ref[...] == segr_ref[...])
    neg_scr[...] = jnp.where(keep, 0.0, -jnp.inf).astype(jnp.float32)


def _fwd_kernel(c_ref, b_ref, segc_ref, segr_ref, x_ref, cumc_ref, cumr_ref, dtr_ref,
                y_ref, s_scr, neg_scr):
    @pl.when(pl.program_id(0) == 0)
    def _():
        _prologue(c_ref, b_ref, segc_ref, segr_ref, s_scr, neg_scr)

    for k in range(PAIR):
        cc = cumc_ref[0, :, k:k + 1]
        cr = cumr_ref[0, k:k + 1, :]
        dr = dtr_ref[0, k:k + 1, :]
        decays = jnp.exp(cc - cr + neg_scr[...])
        mixing = s_scr[...] * (decays * dr)
        y_ref[:, k * HEAD_DIM:(k + 1) * HEAD_DIM] = _dot(
            mixing, x_ref[:, k * HEAD_DIM:(k + 1) * HEAD_DIM])


def _bwd_kernel(c_ref, b_ref, segc_ref, segr_ref, x_ref, cumc_ref, cumr_ref, dtr_ref, g_ref,
                dx_ref, dcumc_ref, dcumr_ref, ddtr_ref, db_ref, dc_ref,
                s_scr, neg_scr, ds_scr):
    step = pl.program_id(0)

    @pl.when(step == 0)
    def _():
        _prologue(c_ref, b_ref, segc_ref, segr_ref, s_scr, neg_scr)
        ds_scr[...] = jnp.zeros_like(ds_scr)

    for k in range(PAIR):
        cc = cumc_ref[0, :, k:k + 1]
        cr = cumr_ref[0, k:k + 1, :]
        dr = dtr_ref[0, k:k + 1, :]
        decays = jnp.exp(cc - cr + neg_scr[...])
        weights = decays * dr
        scores = s_scr[...]
        mixing = scores * weights
        xh = x_ref[:, k * HEAD_DIM:(k + 1) * HEAD_DIM]
        gh = g_ref[:, k * HEAD_DIM:(k + 1) * HEAD_DIM]
        dx_ref[:, k * HEAD_DIM:(k + 1) * HEAD_DIM] = _dot_tn(mixing, gh)
        d_mix = _dot_nt(gh, xh)
        d_dec = d_mix * decays
        ds_scr[...] += d_dec * dr
        through = d_dec * scores
        d_dt_row = jnp.sum(through, axis=0, keepdims=True)
        q_mat = through * dr
        dcumc_ref[0, :, k:k + 1] = jnp.sum(q_mat, axis=1, keepdims=True)
        dcumr_ref[0, k:k + 1, :] = -(d_dt_row * dr)
        ddtr_ref[0, k:k + 1, :] = d_dt_row

    @pl.when(step == pl.num_programs(0) - 1)
    def _():
        dc_ref[...] = _dot(ds_scr[...], b_ref[...])
        db_ref[...] = _dot_tn(ds_scr[...], c_ref[...])


def _specs(rows, state):
    full = lambda shape: pl.BlockSpec(shape, lambda g: (0,) * len(shape))
    return [
        full((rows, state)),
        full((rows, state)),
        full((rows, 1)),
        full((1, rows)),
        pl.BlockSpec((rows, PAIR * HEAD_DIM), lambda g: (0, g)),
        pl.BlockSpec((1, rows, PAIR), lambda g: (g, 0, 0)),
        pl.BlockSpec((1, PAIR, rows), lambda g: (g, 0, 0)),
        pl.BlockSpec((1, PAIR, rows), lambda g: (g, 0, 0)),
    ]


def _prep(dt, cum, seg):
    rows, heads = dt.shape
    groups = heads // PAIR
    cumr = cum.T.reshape(groups, PAIR, rows)
    cumc = jnp.transpose(cumr, (0, 2, 1))
    dtr = dt.T.reshape(groups, PAIR, rows)
    segc = seg.reshape(rows, 1)
    segr = seg.reshape(1, rows)
    return cumc, cumr, dtr, segc, segr


def _fwd_call(x, dt, cum, b_mat, c_mat, seg):
    rows, inner = x.shape
    heads = dt.shape[1]
    groups = heads // PAIR
    state = b_mat.shape[1]
    cumc, cumr, dtr, segc, segr = _prep(dt, cum, seg)
    flops = 2 * rows * rows * state * 6 + heads * (2 * rows * rows * HEAD_DIM * 6 + 8 * rows * rows)
    return pl.pallas_call(
        _fwd_kernel,
        grid=(groups,),
        in_specs=_specs(rows, state),
        out_specs=pl.BlockSpec((rows, PAIR * HEAD_DIM), lambda g: (0, g)),
        out_shape=jax.ShapeDtypeStruct((rows, inner), jnp.float32),
        scratch_shapes=[pltpu.VMEM((rows, rows), jnp.float32),
                        pltpu.VMEM((rows, rows), jnp.float32)],
        compiler_params=pltpu.CompilerParams(dimension_semantics=("arbitrary",)),
        cost_estimate=pl.CostEstimate(flops=flops, transcendentals=heads * rows * rows,
                                      bytes_accessed=4 * (2 * rows * inner + 2 * rows * state)),
        name="ssd_fwd",
    )(c_mat, b_mat, segc, segr, x, cumc, cumr, dtr)


def _bwd_call(x, dt, cum, b_mat, c_mat, seg, g):
    rows, inner = x.shape
    heads = dt.shape[1]
    groups = heads // PAIR
    state = b_mat.shape[1]
    cumc, cumr, dtr, segc, segr = _prep(dt, cum, seg)
    full = lambda shape: pl.BlockSpec(shape, lambda gi: (0,) * len(shape))
    flops = 2 * rows * rows * state * 6 * 3 + heads * (2 * 2 * rows * rows * HEAD_DIM * 6 + 16 * rows * rows)
    dx, dcumc, dcumr, ddtr, db, dc = pl.pallas_call(
        _bwd_kernel,
        grid=(groups,),
        in_specs=_specs(rows, state) + [pl.BlockSpec((rows, PAIR * HEAD_DIM), lambda gi: (0, gi))],
        out_specs=[
            pl.BlockSpec((rows, PAIR * HEAD_DIM), lambda gi: (0, gi)),
            pl.BlockSpec((1, rows, PAIR), lambda gi: (gi, 0, 0)),
            pl.BlockSpec((1, PAIR, rows), lambda gi: (gi, 0, 0)),
            pl.BlockSpec((1, PAIR, rows), lambda gi: (gi, 0, 0)),
            full((rows, state)),
            full((rows, state)),
        ],
        out_shape=[
            jax.ShapeDtypeStruct((rows, inner), jnp.float32),
            jax.ShapeDtypeStruct((groups, rows, PAIR), jnp.float32),
            jax.ShapeDtypeStruct((groups, PAIR, rows), jnp.float32),
            jax.ShapeDtypeStruct((groups, PAIR, rows), jnp.float32),
            jax.ShapeDtypeStruct((rows, state), jnp.float32),
            jax.ShapeDtypeStruct((rows, state), jnp.float32),
        ],
        scratch_shapes=[pltpu.VMEM((rows, rows), jnp.float32),
                        pltpu.VMEM((rows, rows), jnp.float32),
                        pltpu.VMEM((rows, rows), jnp.float32)],
        compiler_params=pltpu.CompilerParams(dimension_semantics=("arbitrary",)),
        cost_estimate=pl.CostEstimate(flops=flops, transcendentals=heads * rows * rows,
                                      bytes_accessed=4 * (4 * rows * inner + 4 * rows * state)),
        name="ssd_bwd",
    )(c_mat, b_mat, segc, segr, x, cumc, cumr, dtr, g)
    d_cum = jnp.transpose(dcumc, (0, 2, 1)).reshape(heads, rows).T + dcumr.reshape(heads, rows).T
    d_dt = ddtr.reshape(heads, rows).T
    return dx, d_dt, d_cum, db, dc


@jax.custom_vjp
def ssd_core(x, dt, cum, b_mat, c_mat, seg):
    return _fwd_call(x, dt, cum, b_mat, c_mat, seg)


def _ssd_core_fwd(x, dt, cum, b_mat, c_mat, seg):
    return _fwd_call(x, dt, cum, b_mat, c_mat, seg), (x, dt, cum, b_mat, c_mat, seg)


def _ssd_core_bwd(res, g):
    x, dt, cum, b_mat, c_mat, seg = res
    dx, d_dt, d_cum, db, dc = _bwd_call(x, dt, cum, b_mat, c_mat, seg, g)
    return dx, d_dt, d_cum, db, dc, None


ssd_core.defvjp(_ssd_core_fwd, _ssd_core_bwd)

from jax.sharding import PartitionSpec as P
from jax.experimental.layout import Layout, with_layout_constraint

NORM_EPS = 1e-05


def contract_rows(first_op, second_op):
    return lax.dot_general(
        first_op, second_op, (((0,), (0,)), ((), ())), preferred_element_type=jnp.float32
    )


def contract_cols(first_op, second_op):
    return lax.dot_general(
        first_op, second_op, (((1,), (1,)), ((), ())), preferred_element_type=jnp.float32
    )


def segment_ids(lengths, row_count):
    seq_ends = jnp.cumsum(lengths)
    positions = jnp.arange(row_count, dtype=jnp.int32)
    return jnp.sum((positions[:, None] >= seq_ends[None, :]).astype(jnp.int32), axis=1)


def causal_conv(signal, kernel_w, kernel_b, segment):
    kernel_len = kernel_w.shape[0]
    row_count = signal.shape[0]
    summed = kernel_b[None, :] + kernel_w[kernel_len - 1][None, :] * signal
    for lag_steps in range(1, kernel_len):
        shifted = jnp.concatenate(
            [jnp.zeros((lag_steps, signal.shape[1]), jnp.float32), signal[: row_count - lag_steps]],
            axis=0,
        )
        earlier = jnp.concatenate(
            [jnp.full((lag_steps,), -1, jnp.int32), segment[: row_count - lag_steps]]
        )
        same_seq = (earlier == segment).astype(signal.dtype)
        summed = (
            summed + kernel_w[kernel_len - 1 - lag_steps][None, :] * shifted * same_seq[:, None]
        )
    return summed


def mixer_core(zx_rows, dt_raw, b_conv, c_conv, conv_wx, conv_bx, a_log, dt_bias, d_skip,
               segment=None):
    inner_n = zx_rows.shape[1] // 2
    heads_n = a_log.shape[0]
    x_conv = jax.nn.silu(causal_conv(zx_rows[:, inner_n:], conv_wx, conv_bx, segment))
    steps_dt = jax.nn.softplus(dt_raw + dt_bias[None, :])
    decay = steps_dt * (-jnp.exp(a_log))[None, :]
    cum = jnp.cumsum(decay, axis=0)
    scanned = ssd_core(x_conv, steps_dt, cum, b_conv, c_conv, segment)
    skip = jnp.repeat(d_skip, inner_n // heads_n)
    mixed_out = scanned + skip[None, :] * x_conv
    return mixed_out * jax.nn.silu(zx_rows[:, :inner_n])


def bc_core(bc_pre, conv_wbc, conv_bbc, segment=None):
    return jax.nn.silu(causal_conv(bc_pre, conv_wbc, conv_bbc, segment))


def per_device_body(tokens, cotangent, seq_lens, input_norm_gain, w_zx, w_bc, w_dt, conv_wx, conv_bx,
               conv_wbc, conv_bbc, a_log, dt_bias, d_skip, norm_gate, w_out):
    n_dp = lax.axis_size("dp")
    x_full = lax.all_gather(tokens, "tensor", axis=1, tiled=True)
    cot_full = lax.all_gather(cotangent, "tensor", axis=1, tiled=True)
    row_count = tokens.shape[0]
    feat_n = tokens.shape[1]
    d_model = x_full.shape[1]
    feat_start = lax.axis_index("tensor") * feat_n
    state_n = w_bc.shape[1] // 2
    inner_loc = norm_gate.shape[0]
    inner_all = inner_loc * lax.axis_size("tensor")
    segment = segment_ids(seq_lens[0], row_count)
    is_live = (segment < seq_lens.shape[1])[:, None]
    w_zx_flat = w_zx.reshape(d_model, 2 * inner_loc)
    tok_float = x_full.astype(jnp.float32)
    inverse_root_mean = lax.rsqrt(jnp.mean(tok_float * tok_float, axis=1, keepdims=True) + NORM_EPS)
    unit_scaled_input = tok_float * inverse_root_mean
    normed = (unit_scaled_input * input_norm_gain[None, :]).astype(jnp.bfloat16)
    zx_rows = jnp.dot(normed, w_zx_flat, preferred_element_type=jnp.float32)
    bc_pre = jnp.dot(normed, w_bc, preferred_element_type=jnp.float32)
    dt_raw = jnp.dot(normed, w_dt, preferred_element_type=jnp.float32)
    bc_post, bc_back = jax.vjp(partial(bc_core, segment=segment), bc_pre, conv_wbc, conv_bbc)
    gated_rows, core_back = jax.vjp(
        partial(mixer_core, segment=segment),
        zx_rows, dt_raw, bc_post[:, :state_n], bc_post[:, state_n:],
        conv_wx, conv_bx, a_log, dt_bias, d_skip,
    )
    cot_live = jnp.where(is_live, cot_full, jnp.zeros_like(cot_full))
    d_gate = contract_cols(cot_live, w_out)
    d_hat = d_gate * norm_gate[None, :]
    stats = lax.psum(
        jnp.concatenate([jnp.sum(gated_rows * gated_rows, axis=1, keepdims=True),
                         jnp.sum(d_hat * gated_rows, axis=1, keepdims=True)], axis=1),
        "tensor")
    squares, cross_sum = stats[:, 0:1], stats[:, 1:2]
    r_gate = lax.rsqrt(squares / inner_all + NORM_EPS)
    gate_hat = gated_rows * r_gate
    gate_out = (gate_hat * norm_gate[None, :]).astype(jnp.bfloat16)
    branch_part = jnp.dot(gate_out, w_out, preferred_element_type=jnp.float32)
    grad_gate = jnp.sum(d_gate * gate_hat, axis=0)
    d_gated = r_gate * d_hat - gated_rows * (r_gate * r_gate * r_gate * cross_sum / inner_all)
    d_gated, branch_part = lax.optimization_barrier((d_gated, branch_part))
    branch = lax.psum_scatter(branch_part, "tensor", scatter_dimension=1, tiled=True)
    own_float = tokens.astype(jnp.float32)
    block_out = (own_float + jnp.where(is_live, branch, 0.0)).astype(jnp.bfloat16)
    d_zx, d_dt, d_b, d_c, grad_conv_wx, grad_conv_bx, grad_a_log, grad_dt_bias, grad_d_skip = (
        core_back(d_gated)
    )
    n_tp = lax.axis_size("tensor")
    d_bc_part = jnp.concatenate([d_b, d_c], axis=1)
    d_zx_half = d_zx.astype(jnp.bfloat16)
    d_dt_half = d_dt.astype(jnp.bfloat16)
    partial_in = contract_cols(d_zx_half, w_zx_flat) + contract_cols(d_dt_half, w_dt)
    bc_w = d_bc_part.shape[1]
    rs_in = jnp.concatenate(
        [partial_in.reshape(row_count, n_tp, feat_n),
         jnp.broadcast_to(d_bc_part[:, None, :], (row_count, n_tp, bc_w))], axis=2,
    ).reshape(row_count, n_tp * (feat_n + bc_w))
    rs_out = lax.psum_scatter(rs_in, "tensor", scatter_dimension=1, tiled=True)
    d_bc_post = rs_out[:, feat_n:]
    d_bc, grad_conv_wbc, grad_conv_bbc = bc_back(d_bc_post)
    d_bc_half = d_bc.astype(jnp.bfloat16)
    own_hat = lax.dynamic_slice_in_dim(unit_scaled_input, feat_start, feat_n, 1)
    own_gain = lax.dynamic_slice_in_dim(input_norm_gain, feat_start, feat_n, 0)
    own_w_bc = lax.dynamic_slice_in_dim(w_bc, feat_start, feat_n, 0)
    own_dn = rs_out[:, :feat_n] + contract_cols(d_bc_half, own_w_bc)
    own_dxhat = own_dn * own_gain[None, :]
    row_inner_product = lax.psum(jnp.sum(own_dxhat * own_hat, axis=1, keepdims=True),
                                 "tensor") / d_model
    grad_in = jnp.sum(own_dn * own_hat, axis=0)
    d_tokens = cotangent.astype(jnp.float32) + inverse_root_mean * (
        own_dxhat - own_hat * row_inner_product
    )
    smalls = (grad_conv_wx, grad_conv_bx, grad_conv_wbc, grad_conv_bbc, grad_a_log,
              grad_dt_bias, grad_d_skip, grad_gate, grad_in)
    flat_small = jnp.concatenate([s.reshape(-1) for s in smalls])
    chunk = d_model // n_dp
    small_cols = -(-flat_small.shape[0] // chunk)
    small_block = jnp.pad(flat_small, (0, small_cols * chunk - flat_small.shape[0])).reshape(
        chunk, small_cols)
    row_major = Layout(major_to_minor=(0, 1))
    grads_main = with_layout_constraint(
        contract_rows(normed, jnp.concatenate([d_zx_half, d_bc_half, d_dt_half], axis=1)),
        row_major)
    grad_out_t = with_layout_constraint(contract_rows(cot_live, gate_out), row_major)
    packed = with_layout_constraint(
        jnp.concatenate([grads_main, grad_out_t, jnp.tile(small_block, (n_dp, 1))], axis=1),
        row_major)
    reduced = lax.psum_scatter(packed, "dp", scatter_dimension=0, tiled=True)
    col = 0
    pieces = []
    for w in (2 * inner_loc, 2 * state_n, w_dt.shape[1], inner_loc):
        pieces.append(reduced[:, col:col + w])
        col += w
    grad_zx_sum, grad_bc_sum, grad_dt_sum, grad_out_t_sum = pieces
    small_sum = reduced[:, col:].reshape(-1)
    outs_small = []
    pos = 0
    for s in smalls:
        outs_small.append(small_sum[pos:pos + s.size].reshape(s.shape))
        pos += s.size
    grad_zx_out = grad_zx_sum.reshape(chunk, 2, inner_loc)
    return (block_out, d_tokens, grad_zx_out, grad_bc_sum, grad_dt_sum, grad_out_t_sum.T,
            *outs_small)


def solution(mesh):
    in_specs = (
        P("dp", "tensor"), P("dp", "tensor"), P("dp", None), P(),
        P(None, None, "tensor"), P(), P(None, "tensor"), P(None, "tensor"), P("tensor"),
        P(), P(), P("tensor"), P("tensor"), P("tensor"), P("tensor"), P("tensor", None),
    )
    out_specs = (
        P("dp", "tensor"), P("dp", "tensor"), P("dp", None, "tensor"), P("dp", None),
        P("dp", "tensor"), P("tensor", "dp"), P(None, "tensor"), P("tensor"), P(), P(),
        P("tensor"), P("tensor"), P("tensor"), P("tensor"), P("tensor"),
    )
    return jax.shard_map(
        per_device_body, mesh=mesh, in_specs=in_specs, out_specs=out_specs, check_vma=False
    )
```

time: 843 us -> 497 us (0.59)
  waiting for transfers between devices: 385 us -> 249 us
  local copies, waits for them, and re-layouts: 178 us -> 66.2 us
  matrix products: 116 us -> 43.4 us
  other arithmetic: 90.7 us -> 37.6 us
  Pallas kernels: 0 us -> 45.7 us
  blocking collectives: 42.4 us -> 30.4 us
    psum x1 -> x0, waiting for transfers between devices: 120 us -> none  [per_device(): lax.psum(partial_in, 'tensor') + contract_cols(d_bc_half, w_bc)]
    dynamic_update_slice x26 -> x0, local copies, waits for them, and re-layouts: 87.3 us -> none  [ssd_scan(): scan_out = lax.scan(one_block, init_state, inputs)[1]]
    dot_general x26 -> x4, matrix products: 79.4 us -> 12.9 us  [the longest x1 4.63 us: per_device_body(): zx_rows = jnp.dot(normed, w_zx_flat, preferred_element_type=jnp.float32)]
    pallas_call x0 -> x2, Pallas kernels: none -> 45.7 us  [the longest x1 29 us: mixer_core(): scanned = ssd_core(x_conv, steps_dt, cum, b_conv, c_conv, segment)]
    dynamic_update_slice x14 -> x0, other arithmetic: 27.5 us -> none  [ssd_scan(): scan_out = lax.scan(one_block, init_state, inputs)[1]]
    unnamed x9 -> x5, waiting for transfers between devices: 25.7 us -> 1.93 us
    concatenate x0 -> x2, local copies, waits for them, and re-layouts: none -> 19 us  [the longest x1 18.9 us: per_device_body(): jnp.concatenate([grads_main, grad_out_t, jnp.tile(small_block, (n_dp, 1))...]
    unnamed x154 -> x140, local copies, waits for them, and re-layouts: 28.6 us -> 16.1 us
  transfers between devices with their start and end apart: 8 -> 5, of which waited for: 7 -> 4; matrix products, arithmetic and copies ran while one was open for 22% -> 16% of each run, Pallas kernels for 0% -> 3%
where the time goes in v1:
time: 497 us; the launch traced here: 488 us
  waiting for transfers between devices  249 us (50%)
  local copies, waits for them, and re-layouts  66.2 us (13%)
  Pallas kernels  45.7 us (9%)
  matrix products  43.4 us (9%)
  other arithmetic  37.6 us (8%)
  blocking collectives  30.4 us (6%)
  between operations  15 us (3%)
    reduce_scatter x1, waiting for transfers between devices, per_device_body(): reduced = lax.psum_scatter(packed, 'dp', scatter_dimension=0, tiled=True)  104 us
    reduce_scatter x1, waiting for transfers between devices, per_device_body(): rs_out = lax.psum_scatter(rs_in, 'tensor', scatter_dimension=1, tiled=True)  80 us
    all_gather x1, waiting for transfers between devices, per_device_body(): x_full = lax.all_gather(tokens, 'tensor', axis=1, tiled=True)  33.2 us
    reduce_scatter x1, waiting for transfers between devices, per_device_body(): lax.psum_scatter(branch_part, 'tensor', scatter_dimension=1, tiled=True)  30.2 us
    pallas_call x1, Pallas kernels, mixer_core(): scanned = ssd_core(x_conv, steps_dt, cum, b_conv, c_conv, segment)  29 us
    psum x1, blocking collectives, per_device_body(): lax.psum(jnp.concatenate([jnp.sum(gated_rows * gated_rows, axis=1, keepdi...  20.1 us
    concatenate x1, local copies, waits for them, and re-layouts, per_device_body(): jnp.concatenate([grads_main, grad_out_t, jnp.tile(small_block, (n_dp, 1))...  18.9 us
    pallas_call x1, Pallas kernels, _fwd_call(): pl.pallas_call(_fwd_kernel, grid=(groups,), in_specs=_specs(rows, state),...  16.7 us
  transfers between devices with their start and end apart: 5, of which 4 were waited for; matrix products, arithmetic and copies ran while one was open for 16% of the time, Pallas kernels for 3%

profile of v1, /device:TPU:0, one launch (start us, length us, event | category | flops | bytes accessed | tf_op | source)
XLA Modules:
  0.0 487.6 jit_solution(1311519445278093623)
XLA Ops:
  7.2 0.7 all-gather.3.cloned.1.call-update
  8.0 0.7 all-gather.5.cloned.1.call-update
  8.8 5.4 %copy.86 = bf16[192,8,2,768]{3,1,2,0:T(8,128)(2,1)} copy(bf16[192,8,2,768]{3,2,1,0:T(2,128)(2,1)} %bitcast.89) | data formatting | bytes 9437184
  14.5 0.9 copy.74.segc_ref
  15.7 33.2 %all-gather.3.cloned.1.call-done = bf16[512,1536]{1,0:T(8,128)(2,1)} async-done(((bf16[512,384]{1,0:T(8,128)(2,1)}), bf16[512,1536]{1,0:T(8,128)(2,1)}) %all-gather.3.cloned.1.call-update) | async-done | bytes 1572880 | tf_op jit(solution)/shard_map/all_gather | solution.py:260
  48.9 1.9 fusion
  50.9 4.6 fusion.42
  55.5 1.4 slice.186
  56.9 1.3 slice.185
  58.3 1.2 slice.184
  59.5 1.4 compare_select_fusion.3
  61.0 1.1 reduce-window.24
  62.5 1.7 copy.75.cumc_ref
  64.3 0.6 reshape.232.dtr_ref
  65.0 2.4 fusion.43
  67.9 0.8 fusion.53
  68.7 1.0 copy-done.3
  69.7 3.0 fusion.12
  72.7 16.7 %jvp_ssd_fwd_.1 = f32[512,768]{1,0:T(8,128)} custom-call(f32[512,128]{1,0:T(8,128)} %get-tuple-element.124.c_ref, f32[512,128]{1,0:T(8,128)} %get-tuple-element.123.b_ref, s32[512,1]{1,0:T(8,128)} %copy.74.segc_ref, s32[1,512]{1,0:T(1,128)} %bitcast.101, f32[512,768]{1,0:T(8,128)} %get-tuple-element.109.x_ref, f32[6,512,2]{2,1,0:T(8,128)} %copy.75.cumc_ref, ...), custom_call_target="tpu_custom_call" | custom-call | flops 2843738112 | bytes 3670016 | tf_op jit(solution)/shard_map/jvp(ssd_fwd)/pallas_call | solution.py:123
  89.4 6.3 %multiply_reduce_fusion.7 = (f32[512]{0:T(512)S(1)}, f32[512]{0:T(512)S(1)}, f32[512,768]{1,0:T(8,128)}, f32[512,768]{1,0:T(8,128)}) fusion(f32[768]{0:T(1024)S(1)} %copy-done.36, f32[512,1536]{1,0:T(8,128)} %copy-done.2, f32[512,768]{1,0:T(8,128)} %jvp_ssd_fwd_.1, f32[512,768]{1,0:T(8,128)} %get-tuple-element.110, f32[768]{0:T(1024)S(1)} %mul.503, ...), kind=kOutput, calls=%fused_computation.32 | convolution fusion | flops 1215036416 | bytes 11807232 | tf_op jit(solution)/shard_map/dot_general | solution.py:209
  95.8 20.1 %psum.14 = f32[512,2]{0,1:T(2,128)S(1)} all-reduce(f32[512,2]{0,1:T(2,128)S(1)} %pad_maximum_fusion.2), channel_id=1, replica_groups=mesh['dp'=8,'tensor'=4] {'tensor'}, use_global_device_ids=true, to_apply=%region_7.8 | all-reduce | flops 1024 | bytes 8192 | tf_op jit(solution)/shard_map/psum | solution.py:288
  115.9 4.5 fusion.41
  120.4 3.1 multiply_reduce_fusion
  123.7 4.4 multiply_reduce_fusion.1
  128.1 29.0 %transpose_jvp_ssd_bwd__.1 = (f32[512,768]{1,0:T(8,128)}, f32[6,512,2]{2,1,0:T(8,128)}, f32[6,2,512]{2,1,0:T(2,128)}, f32[6,2,512]{2,1,0:T(2,128)}, f32[512,128]{1,0:T(8,128)}, /*index=5*/f32[512,128]{1,0:T(8,128)}) custom-call(f32[512,128]{1,0:T(8,128)} %get-tuple-element.124.c_ref, f32[512,128]{1,0:T(8,128)} %get-tuple-element.123.b_ref, ...), custom_call_target="tpu_custom_call" | custom-call | flops 6090129408 | bytes 7340032 | tf_op jit(solution)/shard_map/transpose(jvp(ssd_bwd))/pallas_call | solution.py:247
  157.2 3.9 multiply_reduce_fusion.5
  161.1 0.6 multiply_reduce_fusion.4
  162.2 1.7 copy-done.5
  163.9 1.2 fusion.44
  165.8 4.3 fusion.57
  171.0 5.2 %reduce-window.31 = f32[12,4,128]{2,0,1:T(8,128)S(1)} reduce-window(f32[12,4,128]{2,0,1:T(8,128)S(1)} %copy.80, f32[]{:T(128)} %constant.22.clone.1), window={size=1x1x128 pad=0_0x0_0x0_127}, to_apply=%region_9.10 | reduce-window | flops 780288 | bytes 49156 | tf_op jit(solution)/shard_map/reduce-window.3
  176.7 0.8 fusion.47
  177.5 4.1 convolution_add_fusion
  181.6 4.9 %reshape.235 = f32[512,4,384]{2,1,0:T(4,128)} reshape(f32[512,1536]{1,0:T(8,128)} %convolution_add_fusion) | data formatting | bytes 6291456 | tf_op jit(solution)/shard_map/reshape | solution.py:313
  187.0 1.5 copy-done.12
  188.4 1.1 pad_maximum_fusion
  189.6 2.7 copy.87
  192.9 1.4 dynamic_slice.10
  194.3 0.6 reshape.241
  195.0 0.6 reduce_sum.219
  196.2 6.3 %fusion.13 = f32[1536,768]{1,0:T(8,128)} fusion(bf16[512,1536]{1,0:T(8,128)(2,1)} %all-gather.5.cloned.1.call-done, pred[512]{0:T(512)(128)(4,1)S(1)} %copy-done.49, f32[512,768]{1,0:T(8,128)} %get-tuple-element.108, f32[512]{0:T(512)S(1)} %bitcast.105, f32[768]{0:T(1024)S(1)} %copy-done.37), kind=kOutput, calls=%fused_computation.54 | convolution fusion | flops 1209925632 | bytes 7869952 | tf_op jit(solution)/shard_map/dot_general | solution.py:203
  202.4 1.9 convert_multiply_fusion
  204.3 80.0 %reduce-scatter.6.cloned.1.call-done = f32[512,640]{1,0:T(8,128)} async-done(((f32[512,2560]{1,0:T(8,128)}), f32[512,640]{1,0:T(8,128)}) %reduce-scatter.6.cloned.1.call-update) | async-done | bytes 1310736 | tf_op jit(solution)/shard_map/reduce_scatter | solution.py:316
  284.3 1.3 multiply_reduce_fusion.13
  287.3 1.0 copy-done.20
  288.3 1.7 multiply_reduce_fusion.8
  290.4 7.9 %fusion.1 = f32[1536,1804]{1,0:T(8,128)} fusion(bf16[512,12]{1,0:T(8,128)(2,1)S(1)} %get-tuple-element.91, bf16[512,256]{1,0:T(8,128)(2,1)S(1)} %get-tuple-element.120, bf16[512,1536]{1,0:T(8,128)(2,1)} %copy-done.18, f32[1536]{0:T(1024)S(1)} %copy-done.61, f32[512]{0:T(512)S(1)} %copy-done.33, bf16[512,1536]{1,0:T(8,128)(2,1)S(1)} %copy-done.14), kind=kOutput, calls=%fused_computation.9 | convolution fusion | flops 2846134272 | bytes 14512128 | tf_op jit(solution)/shard_map/dot_general | solution.py:203
  298.3 18.9 %concatenate.66 = f32[1536,2605]{1,0:T(8,128)} concatenate(f32[1536,1804]{1,0:T(8,128)} %fusion.1, f32[1536,768]{1,0:T(8,128)} %fusion.13, f32[1536,33]{1,0:T(8,128)S(1)} %bitcast.94), dimensions={1} | concatenate | bytes 32010240 | tf_op jit(solution)/shard_map/concatenate | solution.py:344
  317.2 30.2 %reduce-scatter.4.cloned.1.call-done = f32[512,384]{1,0:T(8,128)} async-done(((f32[512,1536]{1,0:T(8,128)}), f32[512,384]{1,0:T(8,128)}) %reduce-scatter.4.cloned.1.call-update) | async-done | bytes 786448 | tf_op jit(solution)/shard_map/reduce_scatter | solution.py:300
  347.4 2.1 add_convert_fusion.1
  349.5 10.3 %psum.15 = f32[512,1]{0,1:T(1,128)S(1)} all-reduce(f32[512,1]{0,1:T(1,128)S(1)} %bitcast.116), channel_id=1, replica_groups=mesh['dp'=8,'tensor'=4] {'tensor'}, use_global_device_ids=true, to_apply=%region_13.14 | all-reduce | flops 512 | bytes 4096 | tf_op jit(solution)/shard_map/psum | solution.py:325
  359.8 2.5 multiply_add_fusion.3
  362.3 103.6 %reduce-scatter.8.cloned.1.call-done = f32[192,2605]{1,0:T(8,128)} async-done(((f32[1536,2605]{1,0:T(8,128)}), f32[192,2605]{1,0:T(8,128)}) %reduce-scatter.8.cloned.1.call-update) | async-done | bytes 2000656 | tf_op jit(solution)/shard_map/reduce_scatter | solution.py:346
  465.9 1.0 slice.198
  467.1 0.7 fusion.54
  468.3 0.6 fusion.55
  468.9 0.6 slice.207
  469.6 2.5 slice.194
  472.1 3.0 reshape.248
  475.1 0.7 copy.83
  475.7 0.6 reshape.250
  476.4 0.6 reshape.251
  477.0 1.6 slice.195
  478.6 2.1 slice_bitcast_fusion
  (204 shorter events, 8.9 us)
Async XLA Ops:
  7.2 82.2 %copy-start = (bf16[768,1536]{1,0:T(8,128)(2,1)S(1)}, bf16[768,1536]{1,0:T(8,128)(2,1)}, u32[]{:S(2)}) copy-start(bf16[768,1536]{1,0:T(8,128)(2,1)} %param.31) | copy-start | bytes 7077892
  7.2 41.7 %all-gather.3.cloned.1.call-start = ((), (), s32[]{:S(2)}) async-start(), calls=%async_computation.3 | async-start | bytes 1966080 | tf_op jit(solution)/shard_map/all_gather | solution.py:260
  7.9 81.5 %all-gather.5.cloned.1.call-start = ((), (), s32[]{:S(2)}) async-start(), calls=%async_computation.4 | async-start | bytes 1966080 | tf_op jit(solution)/shard_map/all_gather | solution.py:261
  8.7 275.7 %reduce-scatter.6.cloned.1.call-start = ((), (), s32[]{:S(2)}) async-start(), calls=%async_computation.6 | async-start | bytes 6553600 | tf_op jit(solution)/shard_map/reduce_scatter | solution.py:316
  8.7 5.5 %copy-start.62 = (s32[1,3]{1,0:T(1,128)S(1)}, s32[1,3]{1,0:T(1,128)}, u32[]{:S(2)}) copy-start(s32[1,3]{1,0:T(1,128)} %param.18) | copy-start | bytes 40
  8.7 5.7 %copy-start.52 = (f32[4,256]{1,0:T(4,128)S(1)}, f32[4,256]{1,0:T(4,128)}, u32[]{:S(2)}) copy-start(f32[4,256]{1,0:T(4,128)} %param.25) | copy-start | bytes 12292
  8.7 6.7 %copy-start.39 = (f32[4,768]{1,0:T(4,128)S(1)}, f32[4,768]{1,0:T(4,128)}, u32[]{:S(2)}) copy-start(f32[4,768]{1,0:T(4,128)} %param.23) | copy-start | bytes 36868
  8.8 6.7 %copy-start.64 = (f32[12]{0:T(128)S(1)}, f32[12]{0:T(128)}, u32[]{:S(2)}) copy-start(f32[12]{0:T(128)} %param.27) | copy-start | bytes 148
  8.8 6.7 %copy-start.59 = (f32[12]{0:T(128)S(1)}, f32[12]{0:T(128)}, u32[]{:S(2)}) copy-start(f32[12]{0:T(128)} %param.29) | copy-start | bytes 148
  14.2 36.7 %copy-start.60 = (f32[1536]{0:T(1024)S(1)}, f32[1536]{0:T(1024)}, u32[]{:S(2)}) copy-start(f32[1536]{0:T(1024)} %param.19) | copy-start | bytes 18436
  14.5 41.0 %copy-start.25 = (s32[512]{0:T(512)}, s32[512]{0:T(512)S(1)}, u32[]{:S(2)}) copy-start(s32[512]{0:T(512)S(1)} %convert_reduce_fusion) | copy-start | bytes 6148
  14.5 52.9 %copy-start.40 = (f32[1,256]{1,0:T(1,128)}, f32[1,256]{1,0:T(1,128)S(1)}, u32[]{:S(2)}) copy-start(f32[1,256]{1,0:T(1,128)S(1)} %get-tuple-element.132) | copy-start | bytes 3076
  14.5 52.9 %copy-start.42 = (f32[1,256]{1,0:T(1,128)}, f32[1,256]{1,0:T(1,128)S(1)}, u32[]{:S(2)}) copy-start(f32[1,256]{1,0:T(1,128)S(1)} %get-tuple-element.134) | copy-start | bytes 3076
  14.5 52.9 %copy-start.44 = (f32[1,256]{1,0:T(1,128)}, f32[1,256]{1,0:T(1,128)S(1)}, u32[]{:S(2)}) copy-start(f32[1,256]{1,0:T(1,128)S(1)} %get-tuple-element.135) | copy-start | bytes 3076
  14.5 52.9 %copy-start.46 = (f32[1,256]{1,0:T(1,128)}, f32[1,256]{1,0:T(1,128)S(1)}, u32[]{:S(2)}) copy-start(f32[1,256]{1,0:T(1,128)S(1)} %get-tuple-element.133) | copy-start | bytes 3076
  15.5 44.0 %copy-start.56 = (f32[12]{0:T(128)}, f32[12]{0:T(128)S(1)}, u32[]{:S(2)}) copy-start(f32[12]{0:T(128)S(1)} %exponential_negate_fusion) | copy-start | bytes 148
  15.7 73.7 %copy-start.48 = (pred[512]{0:T(512)(128)(4,1)}, pred[512]{0:T(512)(128)(4,1)S(1)}, u32[]{:S(2)}) copy-start(pred[512]{0:T(512)(128)(4,1)S(1)} %get-tuple-element.139) | copy-start | bytes 1540
  48.9 1.9 copy-start.13
  50.9 14.1 %copy-start.31 = (f32[512]{0:T(512)}, f32[512]{0:T(512)S(1)}, u32[]{:S(2)}) copy-start(f32[512]{0:T(512)S(1)} %add_rsqrt_fusion) | copy-start | bytes 6148
  55.5 2.7 copy-start.2
  62.5 4.9 %copy-start.24 = (f32[6,2,512]{2,1,0:T(2,128)}, f32[6,2,512]{2,1,0:T(2,128)S(1)}, u32[]{:S(2)}) copy-start(f32[6,2,512]{2,1,0:T(2,128)S(1)} %reduce_window_sum.39.cumr_ref) | copy-start | bytes 73732
  62.5 4.9 %copy-start.55 = (f32[256]{0:T(256)S(1)}, f32[256]{0:T(256)}, u32[]{:S(2)}) copy-start(f32[256]{0:T(256)} %param.26) | copy-start | bytes 3076
  65.0 3.7 copy-start.6
  65.0 3.7 copy-start.8
  65.0 3.7 copy-start.10
  67.4 2.3 copy-start.3
  67.4 2.2 copy-start.51
  72.7 16.7 %copy-start.36 = (f32[768]{0:T(1024)S(1)}, f32[768]{0:T(1024)}, u32[]{:S(2)}) copy-start(f32[768]{0:T(1024)} %param.30) | copy-start | bytes 9220
  120.4 3.1 copy-start.4
  120.4 3.3 copy-start.11
  157.1 3.9 copy-start.7
  157.1 3.9 copy-start.9
  162.0 1.9 copy-start.5
  162.0 3.7 slice-start
  163.9 2.0 slice-start.1
  165.8 4.3 copy-start.18
  165.8 4.3 copy-start.16
  170.2 6.3 %copy-start.29 = (f32[6,2,512]{2,1,0:T(2,128)S(1)}, f32[6,2,512]{2,1,0:T(2,128)}, u32[]{:S(2)}) copy-start(f32[6,2,512]{2,1,0:T(2,128)} %get-tuple-element.26) | copy-start | bytes 73732
  170.2 6.5 %copy-start.21 = (f32[512,12]{1,0:T(8,128)S(1)}, f32[512,12]{1,0:T(8,128)}, u32[]{:S(2)}) copy-start(f32[512,12]{1,0:T(8,128)} %get-tuple-element.140) | copy-start | bytes 73732
  170.2 6.5 %copy-start.57 = (f32[12]{0:T(128)S(1)}, f32[12]{0:T(128)}, u32[]{:S(2)}) copy-start(f32[12]{0:T(128)} %copy-done.56) | copy-start | bytes 148
  170.2 7.3 %copy-start.27 = (bf16[1536,12]{0,1:T(8,128)(2,1)S(1)}, bf16[1536,12]{0,1:T(8,128)(2,1)}, u32[]{:S(2)}) copy-start(bf16[1536,12]{0,1:T(8,128)(2,1)} %param.22) | copy-start | bytes 110596
  181.6 4.9 %copy-start.22 = (f32[512,128]{1,0:T(8,128)S(1)}, f32[512,128]{1,0:T(8,128)}, u32[]{:S(2)}) copy-start(f32[512,128]{1,0:T(8,128)} %get-tuple-element.29) | copy-start | bytes 786436
  181.6 4.9 %copy-start.23 = (f32[512,128]{1,0:T(8,128)S(1)}, f32[512,128]{1,0:T(8,128)}, u32[]{:S(2)}) copy-start(f32[512,128]{1,0:T(8,128)} %get-tuple-element.30) | copy-start | bytes 786436
  186.5 1.9 copy-start.12
  192.2 3.4 copy-start.65
  192.3 3.9 copy-start.37
  192.3 3.9 copy-start.49
  192.3 155.1 %reduce-scatter.4.cloned.1.call-start = ((), (), s32[]{:S(2)}) async-start(), calls=%async_computation.5 | async-start | bytes 3932160 | tf_op jit(solution)/shard_map/reduce_scatter | solution.py:300
  192.9 273.0 %reduce-scatter.8.cloned.1.call-start = ((), (), s32[]{:S(2)}) async-start(), calls=%async_computation.7 | async-start | bytes 18579456 | tf_op jit(solution)/shard_map/reduce_scatter | solution.py:346
  196.2 6.3 %copy-start.14 = (bf16[512,1536]{1,0:T(8,128)(2,1)S(1)}, bf16[512,1536]{1,0:T(8,128)(2,1)}, u32[]{:S(2)}) copy-start(bf16[512,1536]{1,0:T(8,128)(2,1)} %all-gather.3.cloned.1.call-done) | copy-start | bytes 4718596
  196.2 6.3 %copy-start.32 = (f32[512]{0:T(512)S(1)}, f32[512]{0:T(512)}, u32[]{:S(2)}) copy-start(f32[512]{0:T(512)} %copy-done.31) | copy-start | bytes 6148
  287.2 2.8 copy-start.28
  287.2 2.8 copy-start.35
  287.2 2.8 copy-start.38
  287.2 2.8 copy-start.53
  287.3 2.8 copy-start.54
  287.3 2.8 copy-start.58
  287.3 3.1 copy-start.33
  287.3 3.1 copy-start.61
  317.2 30.2 %copy-start.17 = (bf16[512,384]{1,0:T(8,128)(2,1)S(1)}, bf16[512,384]{1,0:T(8,128)(2,1)}, u32[]{:S(2)}) copy-start(bf16[512,384]{1,0:T(8,128)(2,1)} %param.16) | copy-start | bytes 1179652
  317.2 30.2 %copy-start.50 = (pred[512]{0:T(512)(128)(4,1)S(1)}, pred[512]{0:T(512)(128)(4,1)}, u32[]{:S(2)}) copy-start(pred[512]{0:T(512)(128)(4,1)} %copy-done.48) | copy-start | bytes 1540
  317.2 42.6 %copy-start.19 = (bf16[512,384]{1,0:T(8,128)(2,1)S(1)}, bf16[512,384]{1,0:T(8,128)(2,1)}, u32[]{:S(2)}) copy-start(bf16[512,384]{1,0:T(8,128)(2,1)} %param.17) | copy-start | bytes 1179652
  469.6 11.1 %copy-start.1 = (bf16[768,1536]{1,0:T(8,128)(2,1)S(1)}, bf16[768,1536]{1,0:T(8,128)(2,1)}, u32[]{:S(2)}) copy-start(bf16[768,1536]{1,0:T(8,128)(2,1)} %param.31) | copy-start | bytes 7077892
  472.1 3.0 slice-start.2
  (10 other events, 10.3 us)
Sparse Core Ops, SparseCore 0:
  9.6 39.3 all-gather.2
  50.5 35.9 all-gather.4
  192.4 91.9 reduce-scatter.5
  286.5 60.8 reduce-scatter.3
  351.0 114.8 reduce-scatter.7

commit v2 on v1

--- a/solution.py
+++ b/solution.py
@@ -304,9 +304,19 @@
         core_back(d_gated)
     )
     n_tp = lax.axis_size("tensor")
-    d_bc_part = jnp.concatenate([d_b, d_c], axis=1)
+    chunk = d_model // n_dp
+    row_major = Layout(major_to_minor=(0, 1))
     d_zx_half = d_zx.astype(jnp.bfloat16)
     d_dt_half = d_dt.astype(jnp.bfloat16)
+    grad_out_t = contract_rows(cot_live, gate_out)
+    grad_z = contract_rows(normed, d_zx_half[:, :inner_loc])
+    (grad_out_t_sum, grad_z_sum), (grad_gate_sum,) = pack_reduce(
+        [grad_out_t, grad_z], [grad_gate], chunk, n_dp, row_major)
+    d_zx, d_dt, block_out, grad_z_sum = lax.optimization_barrier(
+        (d_zx, d_dt, block_out, grad_z_sum))
+    d_zx_half = d_zx.astype(jnp.bfloat16)
+    d_dt_half = d_dt.astype(jnp.bfloat16)
+    d_bc_part = jnp.concatenate([d_b, d_c], axis=1)
     partial_in = contract_cols(d_zx_half, w_zx_flat) + contract_cols(d_dt_half, w_dt)
     bc_w = d_bc_part.shape[1]
     rs_in = jnp.concatenate(
@@ -328,37 +338,41 @@
     d_tokens = cotangent.astype(jnp.float32) + inverse_root_mean * (
         own_dxhat - own_hat * row_inner_product
     )
-    smalls = (grad_conv_wx, grad_conv_bx, grad_conv_wbc, grad_conv_bbc, grad_a_log,
-              grad_dt_bias, grad_d_skip, grad_gate, grad_in)
-    flat_small = jnp.concatenate([s.reshape(-1) for s in smalls])
-    chunk = d_model // n_dp
+    grads_late = contract_rows(
+        normed, jnp.concatenate([d_zx_half[:, inner_loc:], d_bc_half, d_dt_half], axis=1))
+    late_smalls = (grad_conv_wx, grad_conv_bx, grad_conv_wbc, grad_conv_bbc, grad_a_log,
+                   grad_dt_bias, grad_d_skip, grad_in)
+    (grad_late_sum,), late_sums = pack_reduce([grads_late], late_smalls, chunk, n_dp,
+                                              row_major)
+    grad_x_sum = grad_late_sum[:, :inner_loc]
+    grad_bc_sum = grad_late_sum[:, inner_loc:inner_loc + 2 * state_n]
+    grad_dt_sum = grad_late_sum[:, inner_loc + 2 * state_n:]
+    grad_zx_out = jnp.stack([grad_z_sum, grad_x_sum], axis=1)
+    return (block_out, d_tokens, grad_zx_out, grad_bc_sum, grad_dt_sum, grad_out_t_sum.T,
+            *late_sums[:7], grad_gate_sum, late_sums[7])
+
+
+def pack_reduce(mats, smalls, chunk, n_dp, row_major):
+    flat_small = jnp.concatenate([v.reshape(-1) for v in smalls])
     small_cols = -(-flat_small.shape[0] // chunk)
     small_block = jnp.pad(flat_small, (0, small_cols * chunk - flat_small.shape[0])).reshape(
         chunk, small_cols)
-    row_major = Layout(major_to_minor=(0, 1))
-    grads_main = with_layout_constraint(
-        contract_rows(normed, jnp.concatenate([d_zx_half, d_bc_half, d_dt_half], axis=1)),
-        row_major)
-    grad_out_t = with_layout_constraint(contract_rows(cot_live, gate_out), row_major)
     packed = with_layout_constraint(
-        jnp.concatenate([grads_main, grad_out_t, jnp.tile(small_block, (n_dp, 1))], axis=1),
-        row_major)
+        jnp.concatenate([with_layout_constraint(m, row_major) for m in mats]
+                        + [jnp.tile(small_block, (n_dp, 1))], axis=1), row_major)
     reduced = lax.psum_scatter(packed, "dp", scatter_dimension=0, tiled=True)
     col = 0
     pieces = []
-    for w in (2 * inner_loc, 2 * state_n, w_dt.shape[1], inner_loc):
-        pieces.append(reduced[:, col:col + w])
-        col += w
-    grad_zx_sum, grad_bc_sum, grad_dt_sum, grad_out_t_sum = pieces
+    for m in mats:
+        pieces.append(reduced[:, col:col + m.shape[1]])
+        col += m.shape[1]
     small_sum = reduced[:, col:].reshape(-1)
-    outs_small = []
+    outs = []
     pos = 0
-    for s in smalls:
-        outs_small.append(small_sum[pos:pos + s.size].reshape(s.shape))
-        pos += s.size
-    grad_zx_out = grad_zx_sum.reshape(chunk, 2, inner_loc)
-    return (block_out, d_tokens, grad_zx_out, grad_bc_sum, grad_dt_sum, grad_out_t_sum.T,
-            *outs_small)
+    for v in smalls:
+        outs.append(small_sum[pos:pos + v.size].reshape(v.shape))
+        pos += v.size
+    return pieces, outs
 
 
 def solution(mesh):

time: 497 us -> 492 us (0.990)
  other arithmetic: 37.6 us -> 58.7 us
  local copies, waits for them, and re-layouts: 66.2 us -> 52.4 us
  waiting for transfers between devices: 249 us -> 241 us
  matrix products: 43.4 us -> 36.7 us
    reduce_scatter x1, waiting for transfers between devices: 30.2 us -> 0.01 us  [per_device_body(): lax.psum_scatter(branch_part, 'tensor', scatter_dimension=1, tiled=True)]
    concatenate x2 -> x1, local copies, waits for them, and re-layouts: 19 us -> 1.46 us  [pack_reduce(): flat_small = jnp.concatenate([v.reshape(-1) for v in smalls])]
    reduce_scatter x1 -> x2, waiting for transfers between devices: 104 us -> 118 us  [pack_reduce(): reduced = lax.psum_scatter(packed, 'dp', scatter_dimension=0, tiled=True)]
    concatenate x0 -> x2, other arithmetic: none -> 10.5 us  [pack_reduce(): jnp.concatenate([with_layout_constraint(m, row_major) for m in mats] + [j...]
    reduce_scatter x1, waiting for transfers between devices: 80 us -> 88.5 us  [per_device_body(): rs_out = lax.psum_scatter(rs_in, 'tensor', scatter_dimension=1, tiled=True)]
    dot_general x2 -> x3, matrix products: 14.1 us -> 8.31 us  [contract_rows(): lax.dot_general(first_op, second_op, (((0,), (0,)), ((), ())), preferred_...]
    unnamed x140 -> x155, local copies, waits for them, and re-layouts: 16.1 us -> 19.8 us
  transfers between devices with their start and end apart: 5 -> 6, of which waited for: 4 -> 4; matrix products, arithmetic and copies ran while one was open for 16% -> 16% of each run, Pallas kernels for 3% -> 10%
where the time goes in v2:
time: 492 us; the launch traced here: 482 us
  waiting for transfers between devices  241 us (49%)
  other arithmetic  58.7 us (12%)
  local copies, waits for them, and re-layouts  52.4 us (11%)
  Pallas kernels  45.9 us (9%)
  matrix products  36.7 us (7%)
  blocking collectives  32.6 us (7%)
  between operations  15.3 us (3%)
    reduce_scatter x2, waiting for transfers between devices, pack_reduce(): reduced = lax.psum_scatter(packed, 'dp', scatter_dimension=0, tiled=True)  118 us
    reduce_scatter x1, waiting for transfers between devices, per_device_body(): rs_out = lax.psum_scatter(rs_in, 'tensor', scatter_dimension=1, tiled=True)  88.5 us
    all_gather x1, waiting for transfers between devices, per_device_body(): x_full = lax.all_gather(tokens, 'tensor', axis=1, tiled=True)  33.1 us
    pallas_call x1, Pallas kernels, mixer_core(): scanned = ssd_core(x_conv, steps_dt, cum, b_conv, c_conv, segment)  29.1 us
    psum x1, blocking collectives, per_device_body(): lax.psum(jnp.concatenate([jnp.sum(gated_rows * gated_rows, axis=1, keepdi...  21.7 us
    unnamed x155, local copies, waits for them, and re-layouts  19.8 us
    pallas_call x1, Pallas kernels, _fwd_call(): pl.pallas_call(_fwd_kernel, grid=(groups,), in_specs=_specs(rows, state),...  16.7 us
    dot_general x4, matrix products, contract_cols(): lax.dot_general(first_op, second_op, (((1,), (1,)), ((), ())), preferred_...  15.4 us
  transfers between devices with their start and end apart: 6, of which 4 were waited for; matrix products, arithmetic and copies ran while one was open for 16% of the time, Pallas kernels for 10%

profile of v2, /device:TPU:0, one launch (start us, length us, event | category | flops | bytes accessed | tf_op | source)
XLA Modules:
  0.0 482.4 jit_solution(13092326148096368484)
XLA Ops:
  8.0 0.7 all-gather.5.cloned.1.call-update
  8.8 5.5 %copy.89 = bf16[192,8,2,768]{3,1,2,0:T(8,128)(2,1)} copy(bf16[192,8,2,768]{3,2,1,0:T(2,128)(2,1)} %bitcast.93) | data formatting | bytes 9437184
  14.7 0.9 copy.76.segc_ref
  15.9 33.1 %all-gather.3.cloned.1.call-done = bf16[512,1536]{1,0:T(8,128)(2,1)} async-done(((bf16[512,384]{1,0:T(8,128)(2,1)}), bf16[512,1536]{1,0:T(8,128)(2,1)}) %all-gather.3.cloned.1.call-update) | async-done | bytes 1572880 | tf_op jit(solution)/shard_map/all_gather | solution.py:260
  48.9 1.9 fusion
  50.9 4.6 fusion.47
  55.5 1.4 slice.202
  56.9 1.3 slice.201
  58.2 1.3 slice.200
  59.5 1.4 compare_select_fusion.3
  61.0 1.1 reduce-window.24
  62.5 1.6 copy.77.cumc_ref
  64.9 2.4 fusion.48
  67.8 0.8 fusion.58
  68.7 1.0 copy-done.3
  69.6 3.0 fusion.8
  72.6 16.7 %jvp_ssd_fwd_.1 = f32[512,768]{1,0:T(8,128)} custom-call(f32[512,128]{1,0:T(8,128)} %get-tuple-element.134.c_ref, f32[512,128]{1,0:T(8,128)} %get-tuple-element.133.b_ref, s32[512,1]{1,0:T(8,128)} %copy.76.segc_ref, s32[1,512]{1,0:T(1,128)} %bitcast.105, f32[512,768]{1,0:T(8,128)} %get-tuple-element.117.x_ref, f32[6,512,2]{2,1,0:T(8,128)} %copy.77.cumc_ref, ...), custom_call_target="tpu_custom_call" | custom-call | flops 2843738112 | bytes 3670016 | tf_op jit(solution)/shard_map/jvp(ssd_fwd)/pallas_call | solution.py:123
  89.4 6.5 %multiply_reduce_fusion.7 = (f32[512]{0:T(512)S(1)}, f32[512]{0:T(512)S(1)}, f32[512,768]{1,0:T(8,128)}, f32[512,768]{1,0:T(8,128)}) fusion(f32[768]{0:T(1024)S(1)} %copy-done.51, f32[512,1536]{1,0:T(8,128)} %copy-done.2, f32[512,768]{1,0:T(8,128)} %jvp_ssd_fwd_.1, f32[512,768]{1,0:T(8,128)} %get-tuple-element.118, f32[768]{0:T(1024)S(1)} %mul.503, ...), kind=kOutput, calls=%fused_computation.32 | convolution fusion | flops 1215036416 | bytes 11807232 | tf_op jit(solution)/shard_map/dot_general | solution.py:209
  95.9 21.7 %psum.14 = f32[512,2]{0,1:T(2,128)S(1)} all-reduce(f32[512,2]{0,1:T(2,128)S(1)} %pad_maximum_fusion.5), channel_id=1, replica_groups=mesh['dp'=8,'tensor'=4] {'tensor'}, use_global_device_ids=true, to_apply=%region_7.8 | all-reduce | flops 1024 | bytes 8192 | tf_op jit(solution)/shard_map/psum | solution.py:288
  117.6 4.6 fusion.46
  122.1 3.5 multiply_reduce_fusion.5
  125.8 1.2 copy-done.17
  127.0 6.0 %multiply_reduce_fusion = (f32[768]{0:T(1024)}, f32[512,768]{1,0:T(8,128)}, f32[512,768]{1,0:T(8,128)}) fusion(f32[512,768]{1,0:T(8,128)S(1)} %copy-done.17, f32[512,768]{1,0:T(8,128)} %get-tuple-element.27, f32[512,1536]{1,0:T(8,128)} %copy-done.2, f32[512,768]{1,0:T(8,128)} %jvp_ssd_fwd_.1, f32[768]{0:T(1024)S(1)} %copy-done.41), kind=kLoop, calls=%fused_computation.22 | loop fusion | flops 7863552 | bytes 9443328 | tf_op jit(solution)/shard_map/transpose(jvp())/reduce_sum | solution.py:249
  133.0 29.1 %transpose_jvp_ssd_bwd__.1 = (f32[512,768]{1,0:T(8,128)}, f32[6,512,2]{2,1,0:T(8,128)}, f32[6,2,512]{2,1,0:T(2,128)}, f32[6,2,512]{2,1,0:T(2,128)}, f32[512,128]{1,0:T(8,128)}, /*index=5*/f32[512,128]{1,0:T(8,128)}) custom-call(f32[512,128]{1,0:T(8,128)} %get-tuple-element.134.c_ref, f32[512,128]{1,0:T(8,128)} %get-tuple-element.133.b_ref, ...), custom_call_target="tpu_custom_call" | custom-call | flops 6090129408 | bytes 7340032 | tf_op jit(solution)/shard_map/transpose(jvp(ssd_bwd))/pallas_call | solution.py:247
  162.2 4.0 multiply_reduce_fusion.4
  166.2 1.2 multiply_reduce_fusion.3
  168.9 1.7 copy-done.4
  170.6 1.2 fusion.49
  172.6 1.5 fusion.15
  174.5 3.7 fusion.17
  178.2 6.9 %pad_maximum_fusion = f32[1536,1540]{1,0:T(8,128)} fusion(f32[1536,4]{1,0:T(8,128)S(1)} %bitcast.96, f32[1536,768]{1,0:T(8,128)S(1)} %fusion.15, f32[1536,768]{1,0:T(8,128)} %fusion.17), kind=kLoop, calls=%fused_computation | loop fusion | flops 4730880 | bytes 18923520 | tf_op jit(solution)/shard_map/concatenate | solution.py:361
  185.3 1.3 copy-done.22
  187.1 5.2 %reduce-window.31 = f32[12,4,128]{2,0,1:T(8,128)S(1)} reduce-window(f32[12,4,128]{2,0,1:T(8,128)S(1)} %copy.82, f32[]{:T(128)} %constant.19.clone.1), window={size=1x1x128 pad=0_0x0_0x0_127}, to_apply=%region_8.9 | reduce-window | flops 780288 | bytes 49156 | tf_op jit(solution)/shard_map/reduce-window.3
  192.7 0.9 copy.80
  193.5 1.1 pad_maximum_fusion.4
  194.6 1.9 fusion.52
  196.5 3.2 pad_add_fusion
  199.7 2.4 add_convert_fusion
  202.0 66.3 %reduce-scatter.7.cloned.1.call-done = f32[192,1540]{1,0:T(8,128)} async-done(((f32[1536,1540]{1,0:T(8,128)}), f32[192,1540]{1,0:T(8,128)}) %reduce-scatter.7.cloned.1.call-update) | async-done | bytes 1182736 | tf_op jit(solution)/shard_map/reduce_scatter | solution.py:363
  268.3 2.3 slice_bitcast_fusion
  270.6 4.5 fusion.61
  275.2 2.2 convolution_add_fusion
  277.4 4.9 %reshape.239 = f32[512,4,384]{2,1,0:T(4,128)} reshape(f32[512,1536]{1,0:T(8,128)} %convolution_add_fusion) | data formatting | bytes 6291456 | tf_op jit(solution)/shard_map/reshape | solution.py:323
  282.6 3.0 pad_maximum_fusion.2
  285.6 2.6 copy.90
  288.4 1.5 dynamic_slice.10
  291.8 2.0 convert_multiply_fusion
  293.8 88.5 %reduce-scatter.9.cloned.1.call-done = f32[512,640]{1,0:T(8,128)} async-done(((f32[512,2560]{1,0:T(8,128)}), f32[512,640]{1,0:T(8,128)}) %reduce-scatter.9.cloned.1.call-update) | async-done | bytes 1310736 | tf_op jit(solution)/shard_map/reduce_scatter | solution.py:326
  382.3 1.3 multiply_reduce_fusion.13
  384.9 0.7 fusion.50
  386.3 2.2 multiply_reduce_fusion.8
  388.5 1.5 concatenate.69
  390.0 1.3 pad.76
  391.3 1.6 tile.23
  392.9 3.1 fusion.9
  396.1 3.5 pad_maximum_fusion.1
  399.6 0.9 slice-done.1
  400.5 0.7 reshape.255
  401.2 11.0 %psum.15 = f32[512,1]{0,1:T(1,128)S(1)} all-reduce(f32[512,1]{0,1:T(1,128)S(1)} %bitcast.120), channel_id=1, replica_groups=mesh['dp'=8,'tensor'=4] {'tensor'}, use_global_device_ids=true, to_apply=%region_15.16 | all-reduce | flops 512 | bytes 4096 | tf_op jit(solution)/shard_map/psum | solution.py:335
  412.2 2.4 multiply_add_fusion.3
  414.5 51.3 %reduce-scatter.11.cloned.1.call-done = f32[192,1065]{1,0:T(8,128)} async-done(((f32[1536,1065]{1,0:T(8,128)}), f32[192,1065]{1,0:T(8,128)}) %reduce-scatter.11.cloned.1.call-update) | async-done | bytes 817936 | tf_op jit(solution)/shard_map/reduce_scatter | solution.py:363
  465.8 1.0 slice.218
  469.4 1.1 slice_bitcast_fusion.1
  470.6 1.9 copy.85
  (230 shorter events, 16.6 us)
Async XLA Ops:
  7.2 82.2 %copy-start = (bf16[768,1536]{1,0:T(8,128)(2,1)S(1)}, bf16[768,1536]{1,0:T(8,128)(2,1)}, u32[]{:S(2)}) copy-start(bf16[768,1536]{1,0:T(8,128)(2,1)} %param.31) | copy-start | bytes 7077892
  7.2 41.7 %all-gather.3.cloned.1.call-start = ((), (), s32[]{:S(2)}) async-start(), calls=%async_computation.4 | async-start | bytes 1966080 | tf_op jit(solution)/shard_map/all_gather | solution.py:260
  7.9 81.4 %all-gather.5.cloned.1.call-start = ((), (), s32[]{:S(2)}) async-start(), calls=%async_computation.5 | async-start | bytes 1966080 | tf_op jit(solution)/shard_map/all_gather | solution.py:261
  8.7 191.0 %reduce-scatter.5.cloned.1.call-start = ((), (), s32[]{:S(2)}) async-start(), calls=%async_computation.6 | async-start | bytes 3932160 | tf_op jit(solution)/shard_map/reduce_scatter | solution.py:300
  8.7 5.6 %copy-start.71 = (s32[1,3]{1,0:T(1,128)S(1)}, s32[1,3]{1,0:T(1,128)}, u32[]{:S(2)}) copy-start(s32[1,3]{1,0:T(1,128)} %param.18) | copy-start | bytes 40
  8.7 5.9 %copy-start.52 = (f32[4,768]{1,0:T(4,128)S(1)}, f32[4,768]{1,0:T(4,128)}, u32[]{:S(2)}) copy-start(f32[4,768]{1,0:T(4,128)} %param.23) | copy-start | bytes 36868
  8.7 5.9 %copy-start.66 = (f32[4,256]{1,0:T(4,128)S(1)}, f32[4,256]{1,0:T(4,128)}, u32[]{:S(2)}) copy-start(f32[4,256]{1,0:T(4,128)} %param.25) | copy-start | bytes 12292
  8.8 6.8 %copy-start.73 = (f32[12]{0:T(128)S(1)}, f32[12]{0:T(128)}, u32[]{:S(2)}) copy-start(f32[12]{0:T(128)} %param.27) | copy-start | bytes 148
  8.8 6.8 %copy-start.70 = (f32[12]{0:T(128)S(1)}, f32[12]{0:T(128)}, u32[]{:S(2)}) copy-start(f32[12]{0:T(128)} %param.29) | copy-start | bytes 148
  14.3 36.5 %copy-start.32 = (f32[1536]{0:T(1024)S(1)}, f32[1536]{0:T(1024)}, u32[]{:S(2)}) copy-start(f32[1536]{0:T(1024)} %param.19) | copy-start | bytes 18436
  14.6 40.9 %copy-start.28 = (s32[512]{0:T(512)}, s32[512]{0:T(512)S(1)}, u32[]{:S(2)}) copy-start(s32[512]{0:T(512)S(1)} %convert_reduce_fusion) | copy-start | bytes 6148
  14.7 54.0 %copy-start.34 = (f32[768]{0:T(1024)}, f32[768]{0:T(1024)S(1)}, u32[]{:S(2)}) copy-start(f32[768]{0:T(1024)S(1)} %get-tuple-element.94) | copy-start | bytes 9220
  14.7 53.9 %copy-start.36 = (f32[768]{0:T(1024)}, f32[768]{0:T(1024)S(1)}, u32[]{:S(2)}) copy-start(f32[768]{0:T(1024)S(1)} %get-tuple-element.95) | copy-start | bytes 9220
  14.7 53.9 %copy-start.38 = (f32[768]{0:T(1024)}, f32[768]{0:T(1024)S(1)}, u32[]{:S(2)}) copy-start(f32[768]{0:T(1024)S(1)} %get-tuple-element.93) | copy-start | bytes 9220
  14.7 52.6 %copy-start.53 = (f32[1,256]{1,0:T(1,128)}, f32[1,256]{1,0:T(1,128)S(1)}, u32[]{:S(2)}) copy-start(f32[1,256]{1,0:T(1,128)S(1)} %get-tuple-element.140) | copy-start | bytes 3076
  14.7 52.6 %copy-start.55 = (f32[1,256]{1,0:T(1,128)}, f32[1,256]{1,0:T(1,128)S(1)}, u32[]{:S(2)}) copy-start(f32[1,256]{1,0:T(1,128)S(1)} %get-tuple-element.142) | copy-start | bytes 3076
  14.7 52.6 %copy-start.57 = (f32[1,256]{1,0:T(1,128)}, f32[1,256]{1,0:T(1,128)S(1)}, u32[]{:S(2)}) copy-start(f32[1,256]{1,0:T(1,128)S(1)} %get-tuple-element.143) | copy-start | bytes 3076
  14.7 52.6 %copy-start.59 = (f32[1,256]{1,0:T(1,128)}, f32[1,256]{1,0:T(1,128)S(1)}, u32[]{:S(2)}) copy-start(f32[1,256]{1,0:T(1,128)S(1)} %get-tuple-element.141) | copy-start | bytes 3076
  15.6 43.9 %copy-start.68 = (f32[12]{0:T(128)}, f32[12]{0:T(128)S(1)}, u32[]{:S(2)}) copy-start(f32[12]{0:T(128)S(1)} %exponential_negate_fusion) | copy-start | bytes 148
  15.8 73.6 %copy-start.40 = (f32[768]{0:T(1024)}, f32[768]{0:T(1024)S(1)}, u32[]{:S(2)}) copy-start(f32[768]{0:T(1024)S(1)} %mul.503) | copy-start | bytes 9220
  15.9 73.5 %copy-start.61 = (pred[512]{0:T(512)(128)(4,1)}, pred[512]{0:T(512)(128)(4,1)S(1)}, u32[]{:S(2)}) copy-start(pred[512]{0:T(512)(128)(4,1)S(1)} %get-tuple-element.144) | copy-start | bytes 1540
  48.9 1.9 copy-start.5
  55.5 4.0 copy-start.2
  62.5 4.8 copy-start.27
  62.5 4.9 %copy-start.67 = (f32[256]{0:T(256)S(1)}, f32[256]{0:T(256)}, u32[]{:S(2)}) copy-start(f32[256]{0:T(256)} %param.26) | copy-start | bytes 3076
  64.9 3.7 copy-start.10
  64.9 3.8 copy-start.12
  64.9 3.8 copy-start.15
  67.4 2.3 copy-start.3
  67.4 2.2 copy-start.65
  72.6 16.8 %copy-start.51 = (f32[768]{0:T(1024)S(1)}, f32[768]{0:T(1024)}, u32[]{:S(2)}) copy-start(f32[768]{0:T(1024)} %param.30) | copy-start | bytes 9220
  125.6 142.7 %reduce-scatter.7.cloned.1.call-start = ((), (), s32[]{:S(2)}) async-start(), calls=%async_computation.7 | async-start | bytes 11501568 | tf_op jit(solution)/shard_map/reduce_scatter | solution.py:363
  133.0 29.1 %copy-start.16 = (f32[509,768]{1,0:T(8,128)S(1)}, f32[509,768]{1,0:T(8,128)}, u32[]{:S(2)}) copy-start(f32[509,768]{1,0:T(8,128)} %slice.202) | copy-start | bytes 4690948
  162.2 4.0 copy-start.11
  162.2 4.0 copy-start.13
  168.7 1.9 copy-start.4
  170.6 2.0 copy-start.14
  170.6 2.0 copy-start.33
  171.8 2.3 copy-start.8
  172.6 1.9 copy-start.20
  172.6 1.9 copy-start.62
  185.2 1.9 copy-start.43
  185.2 7.5 %copy-start.42 = (f32[6,2,512]{2,1,0:T(2,128)S(1)}, f32[6,2,512]{2,1,0:T(2,128)}, u32[]{:S(2)}) copy-start(f32[6,2,512]{2,1,0:T(2,128)} %get-tuple-element.29) | copy-start | bytes 73732
  185.2 197.0 %reduce-scatter.9.cloned.1.call-start = ((), (), s32[]{:S(2)}) async-start(), calls=%async_computation.8 | async-start | bytes 6553600 | tf_op jit(solution)/shard_map/reduce_scatter | solution.py:326
  187.0 9.4 %copy-start.9 = (f32[512,768]{1,0:T(8,128)S(1)}, f32[512,768]{1,0:T(8,128)}, u32[]{:S(2)}) copy-start(f32[512,768]{1,0:T(8,128)} %copy-done.8) | copy-start | bytes 4718596
  196.5 3.2 copy-start.63
  202.0 68.6 %copy-start.19 = (bf16[512,1536]{1,0:T(8,128)(2,1)S(1)}, bf16[512,1536]{1,0:T(8,128)(2,1)}, u32[]{:S(2)}) copy-start(bf16[512,1536]{1,0:T(8,128)(2,1)} %pad_add_fusion) | copy-start | bytes 4718596
  270.6 4.5 copy-start.30
  288.3 1.6 copy-start.49
  288.3 1.6 copy-start.48
  288.3 2.3 copy-start.47
  288.3 3.0 copy-start.69
  288.3 3.0 copy-start.74
  288.3 3.5 copy-start.7
  288.3 177.5 %reduce-scatter.11.cloned.1.call-start = ((), (), s32[]{:S(2)}) async-start(), calls=%async_computation.9 | async-start | bytes 7962624 | tf_op jit(solution)/shard_map/reduce_scatter | solution.py:363
  385.7 2.9 copy-start.31
  385.7 7.2 %slice-start = ((bf16[512,1536]{1,0:T(8,128)(2,1)}), bf16[512,768]{1,0:T(8,128)(2,1)S(1)}, s32[]{:S(2)}) async-start(bf16[512,1536]{1,0:T(8,128)(2,1)} %pad_add_fusion), calls=%async_computation.10 | async-start | bytes 1572864 | tf_op jit(solution)/shard_map/slice | solution.py:342
  392.9 3.1 copy-start.26
  399.6 12.6 %copy-start.23 = (bf16[512,384]{1,0:T(8,128)(2,1)S(1)}, bf16[512,384]{1,0:T(8,128)(2,1)}, u32[]{:S(2)}) copy-start(bf16[512,384]{1,0:T(8,128)(2,1)} %param.17) | copy-start | bytes 1179652
  399.6 12.6 %copy-start.45 = (f32[384]{0:T(512)S(1)}, f32[384]{0:T(512)}, u32[]{:S(2)}) copy-start(f32[384]{0:T(512)} %dynamic_slice.10) | copy-start | bytes 4612
  414.5 56.0 %copy-start.21 = (f32[192,768]{1,0:T(8,128)S(1)}, f32[192,768]{1,0:T(8,128)}, u32[]{:S(2)}) copy-start(f32[192,768]{1,0:T(8,128)} %get-tuple-element.38) | copy-start | bytes 1769476
  470.5 4.6 copy-start.1
  470.6 1.9 slice-start.2
  470.6 3.8 copy-start.25
  (20 other events, 23.5 us)
Sparse Core Ops, SparseCore 0:
  9.6 39.3 all-gather.2
  50.5 35.9 all-gather.4
  125.8 58.5 reduce-scatter.4
  187.8 80.4 reduce-scatter.6
  288.5 93.7 reduce-scatter.8
  399.8 66.0 reduce-scatter.10
